TPU v7x, 256 devices: a 2x2x32 block of a 4x8x32 slice. The times are simulated.
256 devices in a mesh: replica: 4 (over y, x), tp: 64 (over z, core).
Axes of the slice: x: 2, y: 2, z: 32, core: 2. Of those that a mesh axis runs over, the one named last changes fastest.
The devices are a block of a 4x8x32 slice.
Arguments:
- hidden_in: bfloat16 [16, 16384], P('replica', 'tp'), parts along dimension 0, may hold values from -60 to 60
- norm_gain: bfloat16 [16384], P('tp'), may hold values from 0.5 to 1.5
- w_qkv: bfloat16 [16384, 9216], P(None, 'tp'), may hold values from -0.046875 to 0.046875
- w_out: bfloat16 [8192, 16384], P('tp'), may hold values from -0.1875 to 0.1875
- key_cache: bfloat16 [16, 8192, 512], P('replica', 'tp'), parts along dimension 0, may hold values from -1200 to 1200
- value_cache: bfloat16 [16, 8192, 512], P('replica', 'tp'), parts along dimension 0, may hold values from -6 to 6
- lengths: int32 [16], P('replica'), parts along dimension 0, may hold values from 4096 to 8192
- positions: int32 [16], P('replica'), parts along dimension 0, may hold values from 0 to 16383
Outputs:
- attn_out: bfloat16 [16, 16384], P('replica', 'tp'), parts along dimension 0
- token_scale: float32 [16], P('replica'), parts along dimension 0
There are 4 independent parts, one for each index of `replica`. A program takes and returns all parts, laid end to end along the dimension named above; an argument that names none is the same for every part. Nothing has to cross between parts.
All inputs are finite; a program needn't handle non-finite values.
Results may differ from a plain program's by a relative error of at most 0.017.
The roundings to bfloat16 on the way count: a program that leaves them out, or rounds other values in their place, can miss the bound.
Values may be sent and summed in bfloat16 or wider, within the bound.
A program may use at most 128 MiB of HBM per device.

v0:
```python
import jax
import jax.numpy as jnp
from jax import lax
from jax.sharding import PartitionSpec as P

QUERY_HEADS = 64
KEY_VALUE_HEADS = 4
HEAD_SIZE = 128


def from_everyone(value, axis):
    size = lax.axis_size(axis)
    return lax.all_to_all(
        jnp.broadcast_to(value[None], (size, *value.shape)), axis, 0, 0, tiled=True
    )


def collected_together(value, axis):
    leaves = jax.tree.leaves(value)
    turns = sorted(range(len(leaves)), key=lambda k: -leaves[k].size)
    width = (1, *leaves[turns[0]].shape)[-1]
    lines = [
        jnp.pad(leaves[k].reshape(-1), (0, -leaves[k].size % width)).reshape(-1, width)
        for k in turns
    ]
    both, at, found = (from_everyone(jnp.concatenate(lines), axis), 0, {})
    for k, line in zip(turns, lines):
        slab = both[:, at : at + len(line)].reshape(len(both), -1)
        found[k] = slab[:, : leaves[k].size].reshape(-1, *leaves[k].shape)
        at += len(line)
    numbers = iter(range(len(leaves)))
    return jax.tree.map(lambda _: found[next(numbers)], value)


def folded_in_pairs(pieces, combine):
    while len(jax.tree.leaves(pieces)[0]) > 1:
        pieces = jax.vmap(combine)(
            *(jax.tree.map(lambda part: part[side::2], pieces) for side in (0, 1))
        )
    return jax.tree.map(lambda part: part[0], pieces)


def combined_all(value, axis, combine):
    pieces = collected_together(value, axis)
    return folded_in_pairs(pieces, combine)


def in_order(parts, dim):
    parts = jnp.moveaxis(parts, 0, dim)
    shape = parts.shape
    return parts.reshape(*shape[:dim], shape[dim] * shape[dim + 1], *shape[dim + 2 :])


def gathered_copies(value, axis, dim):
    return in_order(from_everyone(value, axis), dim)


def in_blocks(value, dim, size):
    before, after = (value.shape[:dim], value.shape[dim + 1 :])
    return jnp.moveaxis(value.reshape(*before, size, -1, *after), dim, 0)


def sent_and_summed(value, axis, dim):
    size = lax.axis_size(axis)
    parts = lax.all_to_all(in_blocks(value, dim, size), axis, 0, 0, tiled=True)
    return jnp.sum(parts, axis=0)


def apply_rotation(heads, positions):
    half = HEAD_SIZE // 2
    freq = 500000.0 ** (-(jnp.arange(half, dtype=jnp.float32) * 2.0) / HEAD_SIZE)
    angle = positions.astype(jnp.float32)[:, None] * freq[None, :]
    cosine = jnp.cos(angle)[:, None, :]
    sine = jnp.sin(angle)[:, None, :]
    leading_part = heads[..., :half]
    second = heads[..., half:]
    return jnp.concatenate(
        [leading_part * cosine - second * sine, second * cosine + leading_part * sine], axis=-1
    )


def join_stats(left, right):
    return (left[0] + right[0], jnp.maximum(left[1], right[1]))


def reduce_blocks(parts):
    block_max, block_sum, block_out = parts
    top = jnp.max(block_max, axis=0)
    factor = jnp.exp(block_max - top[None])
    total = jnp.sum(block_sum * factor, axis=0)
    summed = jnp.sum(block_out * factor[..., None], axis=0)
    return (top, total, summed)


def on_device(hidden_in, norm_gain, w_qkv, w_out, key_cache, value_cache, lengths, positions):
    batch_count = hidden_in.shape[0]
    width = w_qkv.shape[0]
    position_range = key_cache.shape[1]
    group_count = QUERY_HEADS // KEY_VALUE_HEADS
    query_width = QUERY_HEADS * HEAD_SIZE
    key_width = KEY_VALUE_HEADS * HEAD_SIZE
    own_heads = w_out.shape[0] // HEAD_SIZE
    inv = 1.0 / HEAD_SIZE**0.5
    values = hidden_in.astype(jnp.float32)
    gained = values * norm_gain.astype(jnp.float32)[None, :]
    squares, gained_peak = combined_all(
        (jnp.sum(values * values, axis=-1), jnp.max(jnp.abs(gained), axis=-1)), "tp", join_stats
    )
    rstd = lax.rsqrt(squares / width + 1e-05)
    normed = gained * rstd[:, None]
    peak = gained_peak * rstd
    token_scale = (peak + 1e-06) / 448.0
    quant = (normed / token_scale[:, None]).astype(jnp.bfloat16)
    local_proj = jnp.dot(gathered_copies(quant, "tp", 1), w_qkv, preferred_element_type=jnp.float32)
    local_proj = (local_proj * token_scale[:, None]).astype(jnp.bfloat16)
    query_key_value = gathered_copies(local_proj, "tp", 1)
    query_rows = apply_rotation(
        query_key_value[:, :query_width]
        .astype(jnp.float32)
        .reshape(batch_count, QUERY_HEADS, HEAD_SIZE),
        positions,
    ).astype(jnp.bfloat16)
    latest_key = apply_rotation(
        query_key_value[:, query_width : query_width + key_width]
        .astype(jnp.float32)
        .reshape(batch_count, KEY_VALUE_HEADS, HEAD_SIZE),
        positions,
    )
    latest_value = (
        query_key_value[:, query_width + key_width :]
        .astype(jnp.float32)
        .reshape(batch_count, KEY_VALUE_HEADS, HEAD_SIZE)
    )
    grouped_query = query_rows.reshape(batch_count, KEY_VALUE_HEADS, group_count, HEAD_SIZE)
    key_rows = key_cache.reshape(batch_count, position_range, KEY_VALUE_HEADS, HEAD_SIZE)
    value_rows = value_cache.reshape(batch_count, position_range, KEY_VALUE_HEADS, HEAD_SIZE)
    scores = (
        jnp.einsum("bgjd,bpgd->bgjp", grouped_query, key_rows, preferred_element_type=jnp.float32)
        * inv
    )
    place = lax.axis_index("tp") * position_range + jnp.arange(position_range, dtype=jnp.int32)
    valid = (place[None, :] < lengths[:, None])[:, None, None, :]
    block_max = jnp.max(jnp.where(valid, scores, -1e30), axis=-1)
    weights = jnp.where(valid, jnp.exp(scores - block_max[..., None]), 0.0)
    block_sum = jnp.sum(weights, axis=-1)
    block_out = jnp.einsum(
        "bgjp,bpgd->bgjd",
        weights.astype(jnp.bfloat16),
        value_rows,
        preferred_element_type=jnp.float32,
    )
    block_max = block_max.reshape(batch_count, QUERY_HEADS)
    block_sum = block_sum.reshape(batch_count, QUERY_HEADS)
    block_out = block_out.reshape(batch_count, QUERY_HEADS, HEAD_SIZE)
    head_start = lax.axis_index("tp") * own_heads
    top, total, summed = reduce_blocks(
        (
            lax.all_to_all(block_max[None], "tp", split_axis=2, concat_axis=0, tiled=True),
            lax.all_to_all(block_sum[None], "tp", split_axis=2, concat_axis=0, tiled=True),
            lax.all_to_all(block_out[None], "tp", split_axis=2, concat_axis=0, tiled=True),
        )
    )
    query_f = grouped_query.astype(jnp.float32)
    score_new = (jnp.einsum("bgjd,bgd->bgj", query_f, latest_key) * inv).reshape(
        batch_count, QUERY_HEADS
    )
    widened_value = jnp.broadcast_to(
        latest_value[:, :, None, :], (batch_count, KEY_VALUE_HEADS, group_count, HEAD_SIZE)
    ).reshape(batch_count, QUERY_HEADS, HEAD_SIZE)
    score_own = lax.dynamic_slice_in_dim(score_new, head_start, own_heads, 1)
    value_own = lax.dynamic_slice_in_dim(widened_value, head_start, own_heads, 1)
    top_new = jnp.maximum(top, score_own)
    keep = jnp.exp(top - top_new)
    fresh = jnp.exp(score_own - top_new)
    total = total * keep + fresh
    summed = summed * keep[..., None] + fresh[..., None] * value_own
    att = (
        (summed / total[..., None]).reshape(batch_count, own_heads * HEAD_SIZE).astype(jnp.bfloat16)
    )
    partial_value = jnp.dot(att, w_out, preferred_element_type=jnp.float32)
    attn_out = sent_and_summed(partial_value, "tp", 1).astype(jnp.bfloat16)
    return (attn_out, token_scale)


def solution(mesh):
    placed = (
        P("replica", "tp"),
        P("tp"),
        P(None, "tp"),
        P("tp", None),
        P("replica", "tp", None),
        P("replica", "tp", None),
        P("replica"),
        P("replica"),
    )
    return jax.shard_map(
        on_device,
        mesh=mesh,
        in_specs=placed,
        out_specs=(P("replica", "tp"), P("replica")),
        check_vma=False,
    )
```

profile of v0, /device:TPU:37, one launch (start us, length us, event | category | flops | bytes accessed | tf_op | source)
XLA Modules:
  0.0 287.6 jit_solution(16955218087965601281)
XLA Ops:
  0.7 0.7 convert_element_type.35
  1.4 0.8 fusion.22
  2.2 59.6 %all_to_all.77 = f32[64,2,4]{2,1,0:T(2,128)S(1)} all-to-all(f32[64,2,4]{2,1,0:T(2,128)S(1)} %broadcast_in_dim.28), channel_id=1, replica_groups=mesh['replica'=4,'tp'=64] {'tp'}, dimensions={0} | all-to-all | bytes 4096 | tf_op jit(solution)/shard_map/all_to_all | solution.py:13
  62.4 0.8 fusion.21
  63.2 36.0 %all_to_all.78 = bf16[64,4,256]{2,1,0:T(4,128)(2,1)S(1)} all-to-all(bf16[64,4,256]{2,1,0:T(4,128)(2,1)S(1)} %broadcast_in_dim.29), channel_id=1, replica_groups=mesh['replica'=4,'tp'=64] {'tp'}, dimensions={0} | all-to-all | bytes 262144 | tf_op jit(solution)/shard_map/all_to_all | solution.py:13
  99.2 3.7 %fusion = bf16[4,144]{1,0:T(4,128)(2,1)S(1)} fusion(bf16[4,16384]{1,0:T(4,128)(2,1)S(1)} %bitcast.130, bf16[16384,144]{0,1:T(8,128)(2,1)} %param.10, f32[4]{0:T(128)S(1)} %get-tuple-element.7), kind=kOutput, calls=%fused_computation.3 | convolution fusion | flops 18875520 | bytes 4850832 | tf_op jit(solution)/shard_map/dot_general | solution.py:114
  102.9 0.7 broadcast_in_dim.30
  103.6 5.6 %all-to-all-start.2 = ((bf16[64,4,144]{2,1,0:T(4,128)(2,1)}), bf16[64,4,144]{2,1,0:T(4,128)(2,1)S(1)}, u32[]{:S(2)}, u32[]{:S(2)}) async-start(bf16[64,4,144]{2,1,0:T(4,128)(2,1)} %broadcast_in_dim.30), calls=%async_computation.2 | async-start | bytes 262144 | tf_op jit(solution)/shard_map/all_to_all | solution.py:13
  109.3 6.5 %copy.38 = bf16[16384,128]{1,0:T(8,128)(2,1)} copy(bf16[16384,128]{0,1:T(8,128)(2,1)} %bitcast.124) | data formatting | bytes 8388608 | tf_op jit(solution)/shard_map/dot_general | solution.py:180
  115.9 23.9 %all-to-all-done.2 = bf16[64,4,144]{2,1,0:T(4,128)(2,1)S(1)} async-done(((bf16[64,4,144]{2,1,0:T(4,128)(2,1)}), bf16[64,4,144]{2,1,0:T(4,128)(2,1)S(1)}, u32[]{:S(2)}, u32[]{:S(2)}) %all-to-all-start.2) | async-done | bytes 73760 | tf_op jit(solution)/shard_map/all_to_all | solution.py:13
  140.2 0.5 select_reduce_fusion
  140.7 0.7 copy.31
  141.4 6.2 %all-to-all-start.4 = ((f32[1,4,64]{1,0,2:T(1,128)}), f32[1,4,64]{1,0,2:T(1,128)S(1)}, u32[]{:S(2)}, u32[]{:S(2)}) async-start(f32[1,4,64]{1,0,2:T(1,128)} %bitcast.15), calls=%async_computation.4 | async-start | bytes 65536 | tf_op jit(solution)/shard_map/all_to_all | solution.py:158
  147.7 0.3 fusion.1
  148.3 0.7 copy.37
  149.0 21.0 %all-to-all-done.4 = f32[1,4,64]{1,0,2:T(1,128)S(1)} async-done(((f32[1,4,64]{1,0,2:T(1,128)}), f32[1,4,64]{1,0,2:T(1,128)S(1)}, u32[]{:S(2)}, u32[]{:S(2)}) %all-to-all-start.4) | async-done | bytes 1056 | tf_op jit(solution)/shard_map/all_to_all | solution.py:158
  170.0 6.2 %all-to-all-start.5 = ((f32[1,4,64]{1,0,2:T(1,128)}), f32[1,4,64]{1,0,2:T(1,128)S(1)}, u32[]{:S(2)}, u32[]{:S(2)}) async-start(f32[1,4,64]{1,0,2:T(1,128)} %bitcast.29), calls=%async_computation.5 | async-start | bytes 65536 | tf_op jit(solution)/shard_map/all_to_all | solution.py:159
  176.2 0.7 copy.30
  177.0 22.1 %all-to-all-done.5 = f32[1,4,64]{1,0,2:T(1,128)S(1)} async-done(((f32[1,4,64]{1,0,2:T(1,128)}), f32[1,4,64]{1,0,2:T(1,128)S(1)}, u32[]{:S(2)}, u32[]{:S(2)}) %all-to-all-start.5) | async-done | bytes 1056 | tf_op jit(solution)/shard_map/all_to_all | solution.py:159
  199.0 5.5 %all-to-all-start.3 = ((f32[1,4,64,128]{3,1,0,2:T(4,128)}), f32[1,4,64,128]{3,1,0,2:T(4,128)S(1)}, u32[]{:S(2)}, u32[]{:S(2)}) async-start(f32[1,4,64,128]{3,1,0,2:T(4,128)} %copy.30), calls=%async_computation.3 | async-start | bytes 262144 | tf_op jit(solution)/shard_map/all_to_all | solution.py:160
  205.2 30.0 %all-to-all-done.3 = f32[1,4,64,128]{3,1,0,2:T(4,128)S(1)} async-done(((f32[1,4,64,128]{3,1,0,2:T(4,128)}), f32[1,4,64,128]{3,1,0,2:T(4,128)S(1)}, u32[]{:S(2)}, u32[]{:S(2)}) %all-to-all-start.3) | async-done | bytes 131104 | tf_op jit(solution)/shard_map/all_to_all | solution.py:160
  235.4 3.4 %convolution_bitcast_fusion = f32[64,4,256]{2,1,0:T(4,128)S(1)} fusion(bf16[64,256,128]{2,1,0:T(8,128)(2,1)} %bitcast.123, f32[4,64,128]{2,0,1:T(4,128)S(1)} %bitcast.135, s32[]{:T(128)S(6)} %select_n.13, f32[4,128]{1,0:T(4,128)S(1)} %fusion.6, f32[4]{0:T(128)S(1)} %get-tuple-element.4, f32[4]{0:T(128)S(1)} %bitcast.144, f32[4]{0:T(128)S(1)} %bitcast.143), kind=kOutput, calls=%fused_computation | convolution fusion | flops 16779776 | bytes 4462084 | tf_op jit(solution)/shard_map/dot_general | solution.py:180
  238.8 48.2 %all_to_all.79 = f32[64,4,256]{2,1,0:T(4,128)S(1)} all-to-all(f32[64,4,256]{2,1,0:T(4,128)S(1)} %convolution_bitcast_fusion), channel_id=1, replica_groups=mesh['replica'=4,'tp'=64] {'tp'}, dimensions={0} | all-to-all | bytes 524288 | tf_op jit(solution)/shard_map/all_to_all | solution.py:65
  287.0 0.7 reduce_sum.55
  (69 shorter events, 2.2 us)
Async XLA Ops:
  0.6 139.6 %copy-start = (bf16[4,128,512]{2,1,0:T(8,128)(2,1)S(1)}, bf16[4,128,512]{2,1,0:T(8,128)(2,1)}, u32[]{:S(2)}) copy-start(bf16[4,128,512]{2,1,0:T(8,128)(2,1)} %param.12) | copy-start | bytes 1572868
  0.6 108.6 %copy-start.3 = (s32[4]{0:T(128)S(1)}, s32[4]{0:T(128)}, u32[]{:S(2)}) copy-start(s32[4]{0:T(128)} %param.15) | copy-start | bytes 52
  62.4 53.4 %copy-start.2 = (f32[4]{0:T(128)}, f32[4]{0:T(128)S(1)}, u32[]{:S(2)}) copy-start(f32[4]{0:T(128)S(1)} %get-tuple-element.7) | copy-start | bytes 52
  103.6 36.2 %all-to-all-start.2 = ((bf16[64,4,144]{2,1,0:T(4,128)(2,1)}), bf16[64,4,144]{2,1,0:T(4,128)(2,1)S(1)}, u32[]{:S(2)}, u32[]{:S(2)}) async-start(bf16[64,4,144]{2,1,0:T(4,128)(2,1)} %broadcast_in_dim.30), calls=%async_computation.2 | async-start | bytes 262144 | tf_op jit(solution)/shard_map/all_to_all | solution.py:13
  109.2 6.5 %copy-start.4 = (s32[4]{0:T(128)S(1)}, s32[4]{0:T(128)}, u32[]{:S(2)}) copy-start(s32[4]{0:T(128)} %param.14) | copy-start | bytes 52
  109.2 38.5 %copy-start.1 = (bf16[4,128,512]{2,1,0:T(8,128)(2,1)S(1)}, bf16[4,128,512]{2,1,0:T(8,128)(2,1)}, u32[]{:S(2)}) copy-start(bf16[4,128,512]{2,1,0:T(8,128)(2,1)} %param.13) | copy-start | bytes 1572868
  141.4 28.5 %all-to-all-start.4 = ((f32[1,4,64]{1,0,2:T(1,128)}), f32[1,4,64]{1,0,2:T(1,128)S(1)}, u32[]{:S(2)}, u32[]{:S(2)}) async-start(f32[1,4,64]{1,0,2:T(1,128)} %bitcast.15), calls=%async_computation.4 | async-start | bytes 65536 | tf_op jit(solution)/shard_map/all_to_all | solution.py:158
  170.0 29.1 %all-to-all-start.5 = ((f32[1,4,64]{1,0,2:T(1,128)}), f32[1,4,64]{1,0,2:T(1,128)S(1)}, u32[]{:S(2)}, u32[]{:S(2)}) async-start(f32[1,4,64]{1,0,2:T(1,128)} %bitcast.29), calls=%async_computation.5 | async-start | bytes 65536 | tf_op jit(solution)/shard_map/all_to_all | solution.py:159
  199.0 36.2 %all-to-all-start.3 = ((f32[1,4,64,128]{3,1,0,2:T(4,128)}), f32[1,4,64,128]{3,1,0,2:T(4,128)S(1)}, u32[]{:S(2)}, u32[]{:S(2)}) async-start(f32[1,4,64,128]{3,1,0,2:T(4,128)} %copy.30), calls=%async_computation.3 | async-start | bytes 262144 | tf_op jit(solution)/shard_map/all_to_all | solution.py:160
where the time goes:
time: 288 us
  blocking collectives  144 us (50%)
  waiting for transfers between devices  97 us (34%)
  starting transfers between devices  23.6 us (8%)
  local copies, waits for them, and re-layouts  10.2 us (4%)
  matrix products  8.09 us (3%)
  other arithmetic  4.06 us (1%)
    all_to_all x2, blocking collectives, from_everyone(): lax.all_to_all(jnp.broadcast_to(value[None], (size, *value.shape)), axis,...  95.6 us
    all_to_all x1, blocking collectives, sent_and_summed(): parts = lax.all_to_all(in_blocks(value, dim, size), axis, 0, 0, tiled=True)  48.2 us
    all_to_all x1, waiting for transfers between devices, on_device(): lax.all_to_all(block_out[None], 'tp', split_axis=2, concat_axis=0, tiled=...  30 us
    all_to_all x1, waiting for transfers between devices, from_everyone(): lax.all_to_all(jnp.broadcast_to(value[None], (size, *value.shape)), axis,...  23.9 us
    all_to_all x1, waiting for transfers between devices, on_device(): lax.all_to_all(block_sum[None], 'tp', split_axis=2, concat_axis=0, tiled=...  22.1 us
    all_to_all x1, waiting for transfers between devices, on_device(): lax.all_to_all(block_max[None], 'tp', split_axis=2, concat_axis=0, tiled=...  21 us
    dot_general x1, local copies, waits for them, and re-layouts, on_device(): partial_value = jnp.dot(att, w_out, preferred_element_type=jnp.float32)  6.45 us
    all_to_all x1, starting transfers between devices, on_device(): lax.all_to_all(block_max[None], 'tp', split_axis=2, concat_axis=0, tiled=...  6.25 us
  transfers between devices with their start and end apart: 4, of which 4 were waited for; matrix products, arithmetic and copies ran while one was open for 3% of the time, Pallas kernels for 0%

commit v1 on v0

v1 whole, which is shorter than its diff:
```python
import functools

import jax
import jax.numpy as jnp
import numpy as np
from jax import lax
from jax.experimental import pallas as pl
from jax.experimental.pallas import tpu as pltpu
from jax.sharding import PartitionSpec as P

QUERY_HEADS = 64
KEY_VALUE_HEADS = 4
HEAD = 128
MESH = pl.DeviceIdType.MESH
F32 = jnp.float32
BF16 = jnp.bfloat16


def sublane():
    return lax.broadcasted_iota(jnp.int32, (8, HEAD), 0)


def half_turn(value):
    return pltpu.roll(value, 4, 0)


def send_all(n, me, source, slots, send_sem, recv_sem):
    half = n // 2

    def push(target):
        pltpu.make_async_remote_copy(
            src_ref=source(target),
            dst_ref=slots.at[me],
            send_sem=send_sem,
            recv_sem=recv_sem,
            device_id={"tp": target},
            device_id_type=MESH,
        ).start()

    push(lax.rem(me + half, n))

    def body(k, _):
        push(lax.rem(me + half - 1 - k, n))
        push(lax.rem(me + half + 1 + k, n))
        return 0

    lax.fori_loop(0, half - 1, body, 0)


def await_bytes(n, slots, sem):
    part = slots.at[pl.ds(0, n - 1)]
    pltpu.make_async_copy(part, part, sem).wait()


def kernel(
    n,
    lengths_ref, positions_ref, freq_ref, hidden_ref, gain_ref, w_qkv_hbm, w_out_hbm, key_hbm, value_hbm,
    out_ref, scale_ref,
    w_qkv, w_out, keys, values,
    mine1, slots1, x_ref, proj_ref, mine2, slots2, q_bf, q_f32, kv_new,
    msg3, slots3, msg4, slots4,
    load_sem, send_sem, recv_sem,
):
    me = lax.axis_index("tp")
    loads = [
        pltpu.make_async_copy(src, dst, load_sem.at[k])
        for k, (src, dst) in enumerate(
            ((w_qkv_hbm, w_qkv), (key_hbm, keys), (value_hbm, values), (w_out_hbm, w_out))
        )
    ]
    for load in loads:
        load.start()

    barrier = pltpu.get_barrier_semaphore()

    def greet(d, _):
        pl.semaphore_signal(barrier, inc=1, device_id={"tp": lax.rem(me + d, n)}, device_id_type=MESH)
        return 0

    lax.fori_loop(1, n, greet, 0)

    sub = sublane()
    upper = sub < 4
    lane = lax.broadcasted_iota(jnp.int32, (8, HEAD), 1)
    token = lax.rem(sub, 4)

    hidden = hidden_ref[...].astype(F32)
    packed = jnp.concatenate([hidden[:, :HEAD], hidden[:, HEAD:]], axis=0).astype(BF16)
    gain = gain_ref[...].astype(F32)
    gain2 = jnp.concatenate([gain[:, :HEAD], gain[:, HEAD:]], axis=0).astype(BF16)
    mine1[0:8, :] = packed
    mine1[8:10, :] = gain2
    slots1[me, 0:8, :] = packed
    slots1[me, 8:10, :] = gain2

    position = jnp.zeros((8, HEAD), F32)
    for b in range(4):
        position = jnp.where(token == b, positions_ref[b].astype(F32), position)
    angle = position * freq_ref[...]
    cosine = jnp.cos(angle)
    sine = jnp.where(lane < HEAD // 2, -jnp.sin(angle), jnp.sin(angle))

    pl.semaphore_wait(barrier, n - 1)

    send_all(n, me, lambda _: mine1, slots1, send_sem.at[0], recv_sem.at[0])
    await_bytes(n, slots1, recv_sem.at[0])

    def gained(s):
        h = slots1[s, 0:8, :].astype(F32)
        g = slots1[s, 8:10, :].astype(F32)
        return h, h * jnp.where(upper, g[0:1, :], g[1:2, :])

    def statistics(s, carry):
        squares, peak = carry
        h, hg = gained(s)
        return squares + h * h, jnp.maximum(peak, jnp.abs(hg))

    squares, peak = lax.fori_loop(
        0, n, statistics, (jnp.zeros((8, HEAD), F32), jnp.zeros((8, HEAD), F32)), unroll=8
    )
    squares = squares + half_turn(squares)
    peak = jnp.maximum(peak, half_turn(peak))
    width = w_qkv.shape[0]
    squares = jnp.broadcast_to(jnp.sum(squares, axis=1, keepdims=True), (8, HEAD))
    peak = jnp.broadcast_to(jnp.max(peak, axis=1, keepdims=True), (8, HEAD))
    rstd = lax.rsqrt(squares / width + 1e-05)
    scale = (peak * rstd + 1e-06) / 448.0
    for b in range(4):
        scale_ref[b] = scale[b, 0]

    def quantize(s, _):
        _, hg = gained(s)
        quant = (hg * rstd) / scale
        x_ref[s] = jnp.concatenate([quant, half_turn(quant)], axis=1).astype(BF16)
        return 0

    lax.fori_loop(0, n, quantize, 0, unroll=8)

    loads[0].wait()
    share = width // n

    def project(s, total):
        rows = pl.ds(pl.multiple_of(s * share, share), share)
        return total + jnp.dot(x_ref[s], w_qkv[rows, :], preferred_element_type=F32)

    columns = w_qkv.shape[1]
    proj = lax.fori_loop(0, n, project, jnp.zeros((8, columns), F32), unroll=8)
    proj_ref[...] = jnp.zeros((8, 2 * HEAD), F32)
    proj_ref[:, :columns] = proj * scale[:, 0:1]
    wide = proj_ref[...]
    turn = lax.rem(me, 8)
    turned = wide
    for k in range(1, 8):
        turned = jnp.where(turn == k, pltpu.roll(wide, 16 * k, 1), turned)
    piece = jnp.where(upper, turned[:, :HEAD], half_turn(turned[:, HEAD:])).astype(BF16)
    mine2[...] = piece
    slots2[me] = piece
    send_all(n, me, lambda _: mine2, slots2, send_sem.at[1], recv_sem.at[1])
    await_bytes(n, slots2, recv_sem.at[1])

    zero = jnp.zeros((8, HEAD), F32)

    def halves(h):
        g, k = h // 9, h % 9
        first = slots2[8 * g + k].astype(F32) if k < 8 else None
        second = slots2[8 * g + k - 1].astype(F32) if k > 0 else None
        return first, second

    def pair(p):
        a0, b0 = halves(2 * p)
        a1, b1 = halves(2 * p + 1)
        low = (a0 if a0 is not None else zero) + (half_turn(b0) if b0 is not None else zero)
        high = (half_turn(a1) if a1 is not None else zero) + (b1 if b1 is not None else zero)
        return jnp.where(upper, low, high)

    def rotated(value):
        return value * cosine + pltpu.roll(value, HEAD // 2, 1) * sine

    for p in range(QUERY_HEADS // 2):
        q = rotated(pair(p)).astype(BF16)
        q_bf[8 * p : 8 * p + 8, :] = q
        q_f32[8 * p : 8 * p + 8, :] = q.astype(F32)
    base = QUERY_HEADS // 2
    for p in range(2):
        kv_new[8 * p : 8 * p + 8, :] = rotated(pair(base + p))
        kv_new[16 + 8 * p : 24 + 8 * p, :] = pair(base + 2 + p)

    inv = 1.0 / HEAD**0.5
    rows = 64
    row_token = lax.rem(lax.broadcasted_iota(jnp.int32, (rows, HEAD), 0), 4)
    place = me * keys.shape[1] + lax.broadcasted_iota(jnp.int32, (rows, HEAD), 1)
    limit = jnp.zeros((rows, HEAD), jnp.int32)
    for b in range(4):
        limit = jnp.where(row_token == b, lengths_ref[b], limit)
    valid = place < limit
    wide_lane = lax.broadcasted_iota(jnp.int32, (rows, HEAD), 1)
    loads[1].wait()
    loads[2].wait()
    for g in range(KEY_VALUE_HEADS):
        q = q_bf[rows * g : rows * g + rows, :]
        heads = slice(HEAD * g, HEAD * g + HEAD)
        scores = jnp.zeros((rows, HEAD), F32)
        for b in range(4):
            part = lax.dot_general(
                q, keys[b, :, heads], (((1,), (1,)), ((), ())), preferred_element_type=F32
            )
            scores = jnp.where(row_token == b, part, scores)
        scores = scores * inv
        top = jnp.max(jnp.where(valid, scores, -1e30), axis=1, keepdims=True)
        weights = jnp.where(valid, jnp.exp(scores - top), 0.0)
        total = jnp.sum(weights, axis=1, keepdims=True)
        rounded = weights.astype(BF16)
        block = jnp.zeros((rows, HEAD), F32)
        for b in range(4):
            part = jnp.dot(rounded, values[b, :, heads], preferred_element_type=F32)
            block = jnp.where(row_token == b, part, block)
        stats = jnp.zeros((rows, HEAD), F32)
        for first, left in ((0, top), (3, total)):
            for k in range(3):
                bits = left.astype(BF16).astype(F32)
                at = 16 * (first + k)
                stats = jnp.where((wide_lane >= at) & (wide_lane < at + 16), bits, stats)
                left = left - bits
        for j in range(rows // 8):
            o = block[8 * j : 8 * j + 8, :]
            t = stats[8 * j : 8 * j + 8, :]
            head = 16 * g + 2 * j
            msg3[head] = jnp.where(upper, o, half_turn(t)).astype(BF16)
            msg3[head + 1] = jnp.where(upper, half_turn(o), t).astype(BF16)
    slots3[me] = msg3[me]
    send_all(n, me, lambda t: msg3.at[t], slots3, send_sem.at[2], recv_sem.at[2])

    def pick(ref, start, index):
        both = ref[pl.ds(pl.multiple_of(start + 8 * (index // 2), 8), 8), :]
        return jnp.where(lax.rem(index, 2) == 1, half_turn(both), both)

    group = me // (QUERY_HEADS // KEY_VALUE_HEADS)
    score_new = jnp.sum(pick(q_f32, 0, me) * pick(kv_new, 0, group), axis=1, keepdims=True) * inv
    score_new = jnp.broadcast_to(score_new, (8, HEAD))
    value_new = pick(kv_new, 16, group)

    spot = lax.broadcasted_iota(jnp.int32, (HEAD, 2 * HEAD), 0)
    side = lax.broadcasted_iota(jnp.int32, (HEAD, 2 * HEAD), 1) // HEAD
    chosen = (spot == 48 * side) | (spot == 48 * side + 16) | (spot == 48 * side + 32)
    spread = jnp.where(chosen, 1.0, 0.0).astype(BF16)
    await_bytes(n, slots3, recv_sem.at[2])
    arrived = slots3[...].reshape(n * 8, HEAD)
    ml = jnp.dot(arrived, spread, preferred_element_type=F32).reshape(n, 8, 2 * HEAD)
    tops = ml[:, :, :HEAD]
    top = half_turn(jnp.max(tops, axis=0))
    summed = jnp.zeros((8, HEAD), F32)
    total = jnp.zeros((8, HEAD), F32)
    for s in range(n):
        factor = jnp.exp(half_turn(tops[s]) - top)
        total = total + half_turn(ml[s, :, HEAD:]) * factor
        summed = summed + slots3[s].astype(F32) * factor
    top_new = jnp.maximum(top, score_new)
    keep = jnp.exp(top - top_new)
    fresh = jnp.exp(score_new - top_new)
    total = total * keep + fresh
    summed = summed * keep + fresh * value_new
    att = jnp.where(upper, summed / total, 0.0).astype(BF16)

    loads[3].wait()
    per = w_out.shape[1] // n
    chunk = 4

    def expand(c, _):
        cols = pl.ds(pl.multiple_of(c * (chunk * per), chunk * per), chunk * per)
        part = jnp.dot(att, w_out[:, cols], preferred_element_type=F32)
        for j in range(chunk):
            left = part[:, j * per : j * per + HEAD]
            right = part[:, j * per + HEAD : (j + 1) * per]
            msg4[c * chunk + j] = jnp.where(upper, left, half_turn(right)).astype(BF16)
        return 0

    lax.fori_loop(0, n // chunk, expand, 0, unroll=4)
    send_all(n, me, lambda t: msg4.at[t], slots4, send_sem.at[3], recv_sem.at[3])
    slots4[me] = msg4[me]
    await_bytes(n, slots4, recv_sem.at[3])

    def gather_sum(s, total):
        return total + slots4[s].astype(F32)

    result = lax.fori_loop(0, n, gather_sum, jnp.zeros((8, HEAD), F32), unroll=8)
    out_ref[:, :HEAD] = result[0:4, :].astype(BF16)
    out_ref[:, HEAD:] = half_turn(result)[0:4, :].astype(BF16)

    await_bytes(n, slots1, send_sem.at[0])
    for k, slots in ((1, slots2), (2, slots3), (3, slots4)):
        await_bytes(n, slots, send_sem.at[k])


def on_device(hidden_in, norm_gain, w_qkv, w_out, key_cache, value_cache, lengths, positions):
    n = lax.axis_size("tp")
    half = HEAD // 2
    freq = np.float32(500000.0 ** (-(np.arange(half, dtype=np.float64) * 2.0) / HEAD))
    freq = jnp.asarray(np.concatenate([freq, freq])[None, :])
    vmem = pl.BlockSpec(memory_space=pltpu.VMEM)
    smem = pl.BlockSpec(memory_space=pltpu.SMEM)
    anywhere = pl.BlockSpec(memory_space=pl.ANY)
    batch = hidden_in.shape[0]
    tile = pltpu.VMEM((n, 8, HEAD), BF16)
    attn_out, token_scale = pl.pallas_call(
        functools.partial(kernel, n),
        out_shape=(
            jax.ShapeDtypeStruct(hidden_in.shape, BF16),
            jax.ShapeDtypeStruct((batch,), F32),
        ),
        in_specs=[smem, smem, vmem, vmem, vmem, anywhere, anywhere, anywhere, anywhere],
        out_specs=(vmem, smem),
        scratch_shapes=[
            pltpu.VMEM(w_qkv.shape, BF16),
            pltpu.VMEM(w_out.shape, BF16),
            pltpu.VMEM(key_cache.shape, BF16),
            pltpu.VMEM(value_cache.shape, BF16),
            pltpu.VMEM((10, HEAD), BF16),
            pltpu.VMEM((n, 10, HEAD), BF16),
            pltpu.VMEM((n, 8, 2 * HEAD), BF16),
            pltpu.VMEM((8, 2 * HEAD), F32),
            pltpu.VMEM((8, HEAD), BF16),
            tile,
            pltpu.VMEM((4 * QUERY_HEADS, HEAD), BF16),
            pltpu.VMEM((4 * QUERY_HEADS, HEAD), F32),
            pltpu.VMEM((32, HEAD), F32),
            tile,
            tile,
            tile,
            tile,
            pltpu.SemaphoreType.DMA((4,)),
            pltpu.SemaphoreType.DMA((4,)),
            pltpu.SemaphoreType.DMA((4,)),
        ],
        compiler_params=pltpu.CompilerParams(collective_id=0, has_side_effects=True),
    )(lengths, positions, freq, hidden_in, norm_gain[None, :], w_qkv, w_out, key_cache, value_cache)
    return attn_out, token_scale


def solution(mesh):
    placed = (
        P("replica", "tp"),
        P("tp"),
        P(None, "tp"),
        P("tp", None),
        P("replica", "tp", None),
        P("replica", "tp", None),
        P("replica"),
        P("replica"),
    )
    return jax.shard_map(
        on_device,
        mesh=mesh,
        in_specs=placed,
        out_specs=(P("replica", "tp"), P("replica")),
        check_vma=False,
    )
```

time: 288 us -> 128 us (0.44)
  blocking collectives: 144 us -> 0 us
  Pallas kernels: 0 us -> 114 us
  waiting for transfers between devices: 97 us -> 0 us
  starting transfers between devices: 23.6 us -> 0 us
  matrix products: 8.09 us -> 0 us
  other arithmetic: 4.06 us -> 0 us
    all_to_all x3 -> x0, blocking collectives: 144 us -> none  [the longest x2 95.6 us: from_everyone(): lax.all_to_all(jnp.broadcast_to(value[None], (size, *value.shape)), axis,...]
    pallas_call x0 -> x1, Pallas kernels: none -> 114 us  [on_device(): pl.pallas_call(functools.partial(kernel, n), out_shape=(jax.ShapeDtypeStr...]
    all_to_all x4 -> x0, waiting for transfers between devices: 97 us -> none  [the longest x1 30 us: on_device(): lax.all_to_all(block_out[None], 'tp', split_axis=2, concat_axis=0, tiled=...]
    all_to_all x4 -> x0, starting transfers between devices: 23.6 us -> none  [the longest x1 6.25 us: on_device(): lax.all_to_all(block_max[None], 'tp', split_axis=2, concat_axis=0, tiled=...]
    unnamed x11 -> x3, local copies, waits for them, and re-layouts: 0.04 us -> 11.6 us
    dot_general x5 -> x0, matrix products: 8.09 us -> none  [the longest x1 3.65 us: on_device(): jnp.dot(gathered_copies(quant, 'tp', 1), w_qkv, preferred_element_type=jn...]
    dot_general x2 -> x0, local copies, waits for them, and re-layouts: 6.55 us -> none  [the longest x1 6.45 us: on_device(): partial_value = jnp.dot(att, w_out, preferred_element_type=jnp.float32)]
  transfers between devices with their start and end apart: 4 -> 0, of which waited for: 4 -> 0; matrix products, arithmetic and copies ran while one was open for 3% -> 0% of each run, Pallas kernels for 0% -> 0%
where the time goes in v1:
time: 128 us
  Pallas kernels  114 us (89%)
  local copies, waits for them, and re-layouts  12.8 us (10%)
    pallas_call x1, Pallas kernels, on_device(): pl.pallas_call(functools.partial(kernel, n), out_shape=(jax.ShapeDtypeStr...  114 us
    unnamed x3, local copies, waits for them, and re-layouts  11.6 us

profile of v1, /device:TPU:37, one launch (start us, length us, event | category | flops | bytes accessed | tf_op | source)
XLA Modules:
  0.0 127.7 jit_solution(315509253751782888)
XLA Ops:
  0.6 1.2 broadcast_in_dim.3.gain_ref
  1.8 9.2 %copy.11.w_qkv_hbm = bf16[16384,144]{1,0:T(8,128)(2,1)} copy(bf16[16384,144]{0,1:T(8,128)(2,1)} %param.11) | data formatting | bytes 9437184 | tf_op args[2]
  11.0 114.3 %shard_map.104 = (bf16[4,256]{1,0:T(4,128)(2,1)}, f32[4]{0:T(128)}) custom-call(s32[4]{0:T(128)} %lengths_ref.1, s32[4]{0:T(128)} %positions_ref.1, f32[1,128]{1,0:T(1,128)} %constant.2.clone.freq_ref, bf16[4,256]{1,0:T(4,128)(2,1)} %hidden_ref.1, bf16[1,256]{1,0:T(2,128)(2,1)} %broadcast_in_dim.3.gain_ref, bf16[16384,144]{1,0:T(8,128)(2,1)} %copy.11.w_qkv_hbm, ...), custom_call_target="tpu_custom_call" | custom-call | tf_op jit(solution)/shard_map/pallas_call | solution.py:304
  125.4 1.3 copy.14
  126.6 1.1 copy.15

commit v2 on v1

v2 whole, which is shorter than its diff:
```python
import functools

import jax
import jax.numpy as jnp
import numpy as np
from jax import lax
from jax.experimental import pallas as pl
from jax.experimental.pallas import tpu as pltpu
from jax.sharding import PartitionSpec as P

QUERY_HEADS = 64
KEY_VALUE_HEADS = 4
HEAD = 128
MESH = pl.DeviceIdType.MESH
F32 = jnp.float32
BF16 = jnp.bfloat16


def sublane():
    return lax.broadcasted_iota(jnp.int32, (8, HEAD), 0)


def half_turn(value):
    return pltpu.roll(value, 4, 0)


def same_core(index, core):
    return {"tp": 2 * index + core}


def send_all(chips, chip, core, pieces, send_sem, recv_sem):
    half = chips // 2

    def push(target):
        for k, (source, landing) in enumerate(pieces):
            pltpu.make_async_remote_copy(
                src_ref=source(target),
                dst_ref=landing,
                send_sem=send_sem.at[k],
                recv_sem=recv_sem.at[k],
                device_id=same_core(target, core),
                device_id_type=MESH,
            ).start()

    push(lax.rem(chip + half, chips))

    def body(k, _):
        push(lax.rem(chip + half - 1 - k, chips))
        push(lax.rem(chip + half + 1 + k, chips))
        return 0

    lax.fori_loop(0, half - 1, body, 0)


def await_bytes(part, sem):
    pltpu.make_async_copy(part, part, sem).wait()


def kernel(
    chips,
    lengths_ref, positions_ref, freq_ref, hidden_ref, gain_ref, w_qkv_hbm, w_out_hbm, key_hbm, value_hbm,
    out_ref, scale_ref,
    w_qkv, w_out, keys, values,
    mine1, mineg, slots1, slotsg, proj_ref, mine2, slots2, q_bf, q_f32, kv_new,
    keep3, give3, got3, msg3, slots3, keep4, give4, got4, msg4, slots4,
    load_sem, send_sem, recv_sem, swap_send, swap_recv,
):
    me = lax.axis_index("tp")
    chip, core = me // 2, lax.rem(me, 2)
    other = 1 - core
    partner = {"tp": me + 1 - 2 * core}

    barrier = pltpu.get_barrier_semaphore()
    pl.semaphore_signal(barrier, inc=1, device_id=partner, device_id_type=MESH)

    def greet(d, _):
        target = same_core(lax.rem(chip + d, chips), core)
        pl.semaphore_signal(barrier, inc=1, device_id=target, device_id_type=MESH)
        return 0

    lax.fori_loop(1, chips, greet, 0)

    def swap(src, dst, k):
        copy = pltpu.make_async_remote_copy(
            src_ref=src,
            dst_ref=dst,
            send_sem=swap_send.at[k],
            recv_sem=swap_recv.at[k],
            device_id=partner,
            device_id_type=MESH,
        )
        copy.start()
        return copy

    sub = sublane()
    upper = sub < 4
    lane = lax.broadcasted_iota(jnp.int32, (8, HEAD), 1)
    token = lax.rem(sub, 4)

    hidden = hidden_ref[...].astype(F32)
    packed = jnp.concatenate([hidden[:, :HEAD], hidden[:, HEAD:]], axis=0).astype(BF16)
    gain = gain_ref[...].astype(F32)
    gain2 = jnp.concatenate([gain[:, :HEAD], gain[:, HEAD:]], axis=0).astype(BF16)
    mine1[...] = packed
    mineg[...] = gain2
    slots1[core, chip] = packed
    slotsg[core, chip] = gain2

    loads = [
        pltpu.make_async_copy(src, dst, load_sem.at[k])
        for k, (src, dst) in enumerate(
            ((w_qkv_hbm, w_qkv), (key_hbm, keys), (value_hbm, values), (w_out_hbm, w_out))
        )
    ]
    for load in loads:
        load.start()

    pl.semaphore_wait(barrier, chips)

    send_all(
        chips, chip, core,
        ((lambda _: mine1, slots1.at[core, chip]), (lambda _: mineg, slotsg.at[core, chip])),
        send_sem.at[0], recv_sem.at[0],
    )

    position = jnp.zeros((8, HEAD), F32)
    for b in range(4):
        position = jnp.where(token == b, positions_ref[b].astype(F32), position)
    angle = position * freq_ref[...]
    cosine = jnp.cos(angle)
    sine = jnp.where(lane < HEAD // 2, -jnp.sin(angle), jnp.sin(angle))

    def rest(slots):
        return slots.at[0, pl.ds(0, chips - 1)]

    await_bytes(rest(slots1), recv_sem.at[0, 0])
    await_bytes(rest(slotsg), recv_sem.at[0, 1])
    swaps = [swap(slots1.at[core], slots1.at[core], 0), swap(slotsg.at[core], slotsg.at[core], 1)]

    def gained(c, s):
        h = slots1[c, s].astype(F32)
        g = slotsg[c, s].astype(F32)
        return h, h * jnp.where(upper, g[0:1, :], g[1:2, :])

    def statistics(c, carry):
        def body(s, carry):
            squares, peak = carry
            h, hg = gained(c, s)
            return squares + h * h, jnp.maximum(peak, jnp.abs(hg))

        return lax.fori_loop(0, chips, body, carry, unroll=8)

    carry = statistics(core, (jnp.zeros((8, HEAD), F32), jnp.zeros((8, HEAD), F32)))
    for copy in swaps:
        copy.wait_recv()
    squares, peak = statistics(other, carry)
    squares = squares + half_turn(squares)
    peak = jnp.maximum(peak, half_turn(peak))
    width = w_qkv.shape[1]
    squares = jnp.broadcast_to(jnp.sum(squares, axis=1, keepdims=True), (8, HEAD))
    peak = jnp.broadcast_to(jnp.max(peak, axis=1, keepdims=True), (8, HEAD))
    rstd = lax.rsqrt(squares / width + 1e-05)
    scale = (peak * rstd + 1e-06) / 448.0
    for b in range(4):
        scale_ref[b] = scale[b, 0]

    loads[0].wait()
    share = width // (2 * chips)

    def project(s, total):
        for c in range(2):
            _, hg = gained(c, s)
            quant = (hg * rstd) / scale
            x = jnp.concatenate([quant, half_turn(quant)], axis=1).astype(BF16)
            rows = pl.ds(pl.multiple_of((2 * s + c) * share, share), share)
            total = total + lax.dot_general(
                x, w_qkv[:, rows], (((1,), (1,)), ((), ())), preferred_element_type=F32
            )
        return total

    columns = w_qkv.shape[0]
    proj = lax.fori_loop(0, chips, project, jnp.zeros((8, columns), F32), unroll=8)
    proj_ref[...] = jnp.zeros((8, 2 * HEAD), F32)
    proj_ref[:, :columns] = proj * scale[:, 0:1]
    wide = proj_ref[...]
    turn = lax.rem(me, 8)
    turned = wide
    for k in range(1, 8):
        turned = jnp.where(turn == k, pltpu.roll(wide, 16 * k, 1), turned)
    piece = jnp.where(upper, turned[:, :HEAD], half_turn(turned[:, HEAD:])).astype(BF16)
    mine2[...] = piece
    slots2[core, chip] = piece
    send_all(
        chips, chip, core, ((lambda _: mine2, slots2.at[core, chip]),), send_sem.at[1], recv_sem.at[1]
    )
    await_bytes(rest(slots2), recv_sem.at[1, 0])
    swaps.append(swap(slots2.at[core], slots2.at[core], 2))
    loads[1].wait()
    loads[2].wait()
    swaps[2].wait_recv()

    zero = jnp.zeros((8, HEAD), F32)

    def arrived2(s):
        return slots2[s % 2, s // 2].astype(F32)

    def halves(h):
        g, k = h // 9, h % 9
        first = arrived2(8 * g + k) if k < 8 else None
        second = arrived2(8 * g + k - 1) if k > 0 else None
        return first, second

    def pair(p):
        a0, b0 = halves(2 * p)
        a1, b1 = halves(2 * p + 1)
        low = (a0 if a0 is not None else zero) + (half_turn(b0) if b0 is not None else zero)
        high = (half_turn(a1) if a1 is not None else zero) + (b1 if b1 is not None else zero)
        return jnp.where(upper, low, high)

    def rotated(value):
        return value * cosine + pltpu.roll(value, HEAD // 2, 1) * sine

    for p in range(QUERY_HEADS // 2):
        q = rotated(pair(p)).astype(BF16)
        q_bf[8 * p : 8 * p + 8, :] = q
        q_f32[8 * p : 8 * p + 8, :] = q.astype(F32)
    base = QUERY_HEADS // 2
    for p in range(2):
        kv_new[8 * p : 8 * p + 8, :] = rotated(pair(base + p))
        kv_new[16 + 8 * p : 24 + 8 * p, :] = pair(base + 2 + p)

    inv = 1.0 / HEAD**0.5
    rows = 64
    row_token = lax.rem(lax.broadcasted_iota(jnp.int32, (rows, HEAD), 0), 4)
    place = me * keys.shape[1] + lax.broadcasted_iota(jnp.int32, (rows, HEAD), 1)
    limit = jnp.zeros((rows, HEAD), jnp.int32)
    for b in range(4):
        limit = jnp.where(row_token == b, lengths_ref[b], limit)
    valid = place < limit
    wide_left = lax.broadcasted_iota(jnp.int32, (rows, HEAD), 1) < HEAD // 2
    even_core = core == 0
    first_swap = len(swaps)
    for g in range(KEY_VALUE_HEADS):
        q = q_bf[rows * g : rows * g + rows, :]
        heads = slice(HEAD * g, HEAD * g + HEAD)
        scores = jnp.zeros((rows, HEAD), F32)
        for b in range(4):
            part = lax.dot_general(
                q, keys[b, :, heads], (((1,), (1,)), ((), ())), preferred_element_type=F32
            )
            scores = jnp.where(row_token == b, part, scores)
        scores = scores * inv
        top = jnp.max(jnp.where(valid, scores, -1e30), axis=1, keepdims=True)
        weights = jnp.where(valid, jnp.exp(scores - top), 0.0)
        total = jnp.sum(weights, axis=1, keepdims=True)
        rounded = weights.astype(BF16)
        block = jnp.zeros((rows, HEAD), F32)
        for b in range(4):
            part = jnp.dot(rounded, values[b, :, heads], preferred_element_type=F32)
            block = jnp.where(row_token == b, part, block)
        stats = jnp.where(wide_left, top, total)
        for j in range(rows // 16):
            at = 4 * g + j
            for k, value in enumerate((block, stats)):
                one, two = value[16 * j : 16 * j + 8, :], value[16 * j + 8 : 16 * j + 16, :]
                evens = jnp.where(upper, one, half_turn(two))
                odds = jnp.where(upper, half_turn(one), two)
                keep3[at, k] = jnp.where(even_core, evens, odds)
                give3[at, k] = jnp.where(even_core, odds, evens)
        part = pl.ds(4 * g, 4)
        swaps.append(swap(give3.at[part], got3.at[part], 3 + g))

    def pick(ref, start, index):
        both = ref[pl.ds(pl.multiple_of(start + 8 * (index // 2), 8), 8), :]
        return jnp.where(lax.rem(index, 2) == 1, half_turn(both), both)

    group = me // (QUERY_HEADS // KEY_VALUE_HEADS)
    score_new = jnp.sum(pick(q_f32, 0, me) * pick(kv_new, 0, group), axis=1, keepdims=True) * inv
    score_new = jnp.broadcast_to(score_new, (8, HEAD))
    value_new = pick(kv_new, 16, group)

    left_half = lane < HEAD // 2

    def both_stats(value):
        turned = pltpu.roll(value, HEAD // 2, 1)
        return jnp.where(left_half, value, turned), jnp.where(left_half, turned, value)

    for g in range(KEY_VALUE_HEADS):
        swaps[first_swap + g].wait_recv()
        for j in range(4):
            at = 4 * g + j
            m0, l0 = both_stats(keep3[at, 1])
            m1, l1 = both_stats(got3[at, 1])
            top = jnp.maximum(m0, m1)
            f0, f1 = jnp.exp(m0 - top), jnp.exp(m1 - top)
            total = l0 * f0 + l1 * f1
            block = keep3[at, 0] * f0 + got3[at, 0] * f1
            stats = zero
            for first, left in ((0, top), (3, total)):
                for k in range(3):
                    bits = left.astype(BF16).astype(F32)
                    here = lane >= 16 * (first + k)
                    stats = jnp.where(here, bits, stats)
                    left = left - bits
            stats = jnp.where(lane >= 96, 0.0, stats)
            msg3[2 * at] = jnp.where(upper, block, half_turn(stats)).astype(BF16)
            msg3[2 * at + 1] = jnp.where(upper, half_turn(block), stats).astype(BF16)
    send_all(
        chips, chip, core, ((lambda t: msg3.at[t], slots3.at[chip]),), send_sem.at[2], recv_sem.at[2]
    )
    slots3[chip] = msg3[chip]

    spot = lax.broadcasted_iota(jnp.int32, (HEAD, 2 * HEAD), 0)
    side = lax.broadcasted_iota(jnp.int32, (HEAD, 2 * HEAD), 1) // HEAD
    chosen = (spot == 48 * side) | (spot == 48 * side + 16) | (spot == 48 * side + 32)
    spread = jnp.where(chosen, 1.0, 0.0).astype(BF16)
    loads[3].wait()
    await_bytes(slots3.at[pl.ds(0, chips - 1)], recv_sem.at[2, 0])
    ml = jnp.dot(slots3[...].reshape(chips * 8, HEAD), spread, preferred_element_type=F32)
    ml = ml.reshape(chips, 8, 2 * HEAD)
    tops = ml[:, :, :HEAD]
    top = half_turn(jnp.max(tops, axis=0))
    summed = zero
    total = zero
    for s in range(chips):
        factor = jnp.exp(half_turn(tops[s]) - top)
        total = total + half_turn(ml[s, :, HEAD:]) * factor
        summed = summed + slots3[s].astype(F32) * factor
    top_new = jnp.maximum(top, score_new)
    keep = jnp.exp(top - top_new)
    fresh = jnp.exp(score_new - top_new)
    total = total * keep + fresh
    summed = summed * keep + fresh * value_new
    att = jnp.where(upper, summed / total, 0.0).astype(BF16)

    per = w_out.shape[1] // (2 * chips)

    def expand(side, dest):
        def body(t, _):
            cols = pl.ds(pl.multiple_of((2 * t + side) * per, per), per)
            part = jnp.dot(att, w_out[:, cols], preferred_element_type=F32)
            dest[t] = jnp.where(upper, part[:, :HEAD], half_turn(part[:, HEAD:]))
            return 0

        lax.fori_loop(0, chips, body, 0, unroll=8)

    expand(other, give4)
    last = swap(give4, got4, 3 + KEY_VALUE_HEADS)
    expand(core, keep4)
    last.wait_recv()

    def merge(t, _):
        msg4[t] = (keep4[t] + got4[t]).astype(BF16)
        return 0

    lax.fori_loop(0, chips, merge, 0, unroll=8)
    send_all(
        chips, chip, core, ((lambda t: msg4.at[t], slots4.at[chip]),), send_sem.at[3], recv_sem.at[3]
    )
    slots4[chip] = msg4[chip]
    await_bytes(slots4.at[pl.ds(0, chips - 1)], recv_sem.at[3, 0])

    def gather_sum(s, total):
        return total + slots4[s].astype(F32)

    result = lax.fori_loop(0, chips, gather_sum, zero, unroll=8)
    out_ref[:, :HEAD] = result[0:4, :].astype(BF16)
    out_ref[:, HEAD:] = half_turn(result)[0:4, :].astype(BF16)

    await_bytes(rest(slots1), send_sem.at[0, 0])
    await_bytes(rest(slotsg), send_sem.at[0, 1])
    await_bytes(rest(slots2), send_sem.at[1, 0])
    await_bytes(slots3.at[pl.ds(0, chips - 1)], send_sem.at[2, 0])
    await_bytes(slots4.at[pl.ds(0, chips - 1)], send_sem.at[3, 0])
    for copy in (*swaps, last):
        copy.wait_send()


def on_device(hidden_in, norm_gain, w_qkv, w_out, key_cache, value_cache, lengths, positions):
    chips = lax.axis_size("tp") // 2
    half = HEAD // 2
    freq = np.float32(500000.0 ** (-(np.arange(half, dtype=np.float64) * 2.0) / HEAD))
    freq = jnp.asarray(np.concatenate([freq, freq])[None, :])
    vmem = pl.BlockSpec(memory_space=pltpu.VMEM)
    smem = pl.BlockSpec(memory_space=pltpu.SMEM)
    anywhere = pl.BlockSpec(memory_space=pl.ANY)
    batch = hidden_in.shape[0]
    tiles = pltpu.VMEM((chips, 8, HEAD), BF16)
    tiles_f32 = pltpu.VMEM((chips, 8, HEAD), F32)
    stats = pltpu.VMEM((chips // 2, 2, 8, HEAD), F32)
    attn_out, token_scale = pl.pallas_call(
        functools.partial(kernel, chips),
        out_shape=(
            jax.ShapeDtypeStruct(hidden_in.shape, BF16),
            jax.ShapeDtypeStruct((batch,), F32),
        ),
        in_specs=[smem, smem, vmem, vmem, vmem, anywhere, anywhere, anywhere, anywhere],
        out_specs=(vmem, smem),
        scratch_shapes=[
            pltpu.VMEM(w_qkv.shape[::-1], BF16),
            pltpu.VMEM(w_out.shape, BF16),
            pltpu.VMEM(key_cache.shape, BF16),
            pltpu.VMEM(value_cache.shape, BF16),
            pltpu.VMEM((8, HEAD), BF16),
            pltpu.VMEM((2, HEAD), BF16),
            pltpu.VMEM((2, chips, 8, HEAD), BF16),
            pltpu.VMEM((2, chips, 2, HEAD), BF16),
            pltpu.VMEM((8, 2 * HEAD), F32),
            pltpu.VMEM((8, HEAD), BF16),
            pltpu.VMEM((2, chips, 8, HEAD), BF16),
            pltpu.VMEM((4 * QUERY_HEADS, HEAD), BF16),
            pltpu.VMEM((4 * QUERY_HEADS, HEAD), F32),
            pltpu.VMEM((32, HEAD), F32),
            stats,
            stats,
            stats,
            tiles,
            tiles,
            tiles_f32,
            tiles_f32,
            tiles_f32,
            tiles,
            tiles,
            pltpu.SemaphoreType.DMA((4,)),
            pltpu.SemaphoreType.DMA((4, 2)),
            pltpu.SemaphoreType.DMA((4, 2)),
            pltpu.SemaphoreType.DMA((4 + KEY_VALUE_HEADS,)),
            pltpu.SemaphoreType.DMA((4 + KEY_VALUE_HEADS,)),
        ],
        compiler_params=pltpu.CompilerParams(collective_id=0, has_side_effects=True),
    )(lengths, positions, freq, hidden_in, norm_gain[None, :], w_qkv.T, w_out, key_cache, value_cache)
    return attn_out, token_scale


def solution(mesh):
    placed = (
        P("replica", "tp"),
        P("tp"),
        P(None, "tp"),
        P("tp", None),
        P("replica", "tp", None),
        P("replica", "tp", None),
        P("replica"),
        P("replica"),
    )
    return jax.shard_map(
        on_device,
        mesh=mesh,
        in_specs=placed,
        out_specs=(P("replica", "tp"), P("replica")),
        check_vma=False,
    )
```

time: 128 us -> 96.7 us (0.76)
  Pallas kernels: 114 us -> 91.1 us
  local copies, waits for them, and re-layouts: 12.8 us -> 3.61 us
    pallas_call x1, Pallas kernels: 114 us -> 91.1 us  [on_device(): pl.pallas_call(functools.partial(kernel, chips), out_shape=(jax.ShapeDtyp...]
    unnamed x3 -> x2, local copies, waits for them, and re-layouts: 11.6 us -> 2.39 us
where the time goes in v2:
time: 96.7 us; the launch traced here: 95.3 us
  Pallas kernels  91.1 us (94%)
  local copies, waits for them, and re-layouts  3.61 us (4%)
    pallas_call x1, Pallas kernels, on_device(): pl.pallas_call(functools.partial(kernel, chips), out_shape=(jax.ShapeDtyp...  91.1 us
    unnamed x2, local copies, waits for them, and re-layouts  2.39 us

profile of v2, /device:TPU:37, one launch (start us, length us, event | category | flops | bytes accessed | tf_op | source)
XLA Modules:
  0.0 95.3 jit_solution(16613733956471996558)
XLA Ops:
  0.6 1.2 %broadcast_in_dim.3.gain_ref = bf16[1,256]{1,0:T(2,128)(2,1)} reshape(bf16[256]{0:T(256)(128)(2,1)} %param.10) | data formatting | bytes 1024 | tf_op jit(solution)/shard_map/broadcast_in_dim | solution.py:431
  1.8 91.1 %shard_map.104 = (bf16[4,256]{1,0:T(4,128)(2,1)}, f32[4]{0:T(128)}) custom-call(s32[4]{0:T(128)} %lengths_ref.1, s32[4]{0:T(128)} %positions_ref.1, f32[1,128]{1,0:T(1,128)} %constant.2.clone.freq_ref, bf16[4,256]{1,0:T(4,128)(2,1)} %hidden_ref.1, bf16[1,256]{1,0:T(2,128)(2,1)} %broadcast_in_dim.3.gain_ref, bf16[144,16384]{1,0:T(8,128)(2,1)} %bitcast.1, ...), custom_call_target="tpu_custom_call" | custom-call | tf_op jit(solution)/shard_map/pallas_call | solution.py:391
  92.9 1.3 %copy.13 = bf16[4,256]{1,0:T(4,128)(2,1)} copy(bf16[4,256]{1,0:T(4,128)(2,1)} %get-tuple-element.4) | data formatting | bytes 4096
  94.2 1.1 %copy.14 = f32[4]{0:T(128)} copy(f32[4]{0:T(128)} %get-tuple-element.5) | data formatting | bytes 32

commit v3 on v2

--- a/solution.py
+++ b/solution.py
@@ -28,28 +28,17 @@
     return {"tp": 2 * index + core}
 
 
-def send_all(chips, chip, core, pieces, send_sem, recv_sem):
-    half = chips // 2
-
-    def push(target):
-        for k, (source, landing) in enumerate(pieces):
-            pltpu.make_async_remote_copy(
-                src_ref=source(target),
-                dst_ref=landing,
-                send_sem=send_sem.at[k],
-                recv_sem=recv_sem.at[k],
-                device_id=same_core(target, core),
-                device_id_type=MESH,
-            ).start()
-
-    push(lax.rem(chip + half, chips))
-
-    def body(k, _):
-        push(lax.rem(chip + half - 1 - k, chips))
-        push(lax.rem(chip + half + 1 + k, chips))
-        return 0
-
-    lax.fori_loop(0, half - 1, body, 0)
+def remote(src, dst, send_sem, recv_sem, target):
+    copy = pltpu.make_async_remote_copy(
+        src_ref=src,
+        dst_ref=dst,
+        send_sem=send_sem,
+        recv_sem=recv_sem,
+        device_id=target,
+        device_id_type=MESH,
+    )
+    copy.start()
+    return copy
 
 
 def await_bytes(part, sem):
@@ -58,83 +47,104 @@
 
 def kernel(
     chips,
-    lengths_ref, positions_ref, freq_ref, hidden_ref, gain_ref, w_qkv_hbm, w_out_hbm, key_hbm, value_hbm,
+    lengths_hbm, positions_hbm, freq_hbm, hidden_hbm, gain_hbm, w_qkv_hbm, w_out_hbm, key_hbm, value_hbm,
     out_ref, scale_ref,
-    w_qkv, w_out, keys, values,
+    w_qkv, w_out, keys, values, lengths_ref, positions_ref, freq_ref, hidden_ref, gain_ref,
     mine1, mineg, slots1, slotsg, proj_ref, mine2, slots2, q_bf, q_f32, kv_new,
     keep3, give3, got3, msg3, slots3, keep4, give4, got4, msg4, slots4,
-    load_sem, send_sem, recv_sem, swap_send, swap_recv,
+    load_sem, send_sem, near_sem, recv_sem, swap_send, swap_recv,
 ):
     me = lax.axis_index("tp")
     chip, core = me // 2, lax.rem(me, 2)
     other = 1 - core
     partner = {"tp": me + 1 - 2 * core}
+    reach = chips // 4
+
+    def ahead(d):
+        return lax.rem(chip + d + chips, chips)
 
     barrier = pltpu.get_barrier_semaphore()
+    for d in range(reach, 0, -1):
+        for target in (ahead(d), ahead(-d)):
+            pl.semaphore_signal(
+                barrier, inc=1, device_id=same_core(target, core), device_id_type=MESH
+            )
     pl.semaphore_signal(barrier, inc=1, device_id=partner, device_id_type=MESH)
 
-    def greet(d, _):
-        target = same_core(lax.rem(chip + d, chips), core)
-        pl.semaphore_signal(barrier, inc=1, device_id=target, device_id_type=MESH)
-        return 0
-
-    lax.fori_loop(1, chips, greet, 0)
+    loads = [
+        pltpu.make_async_copy(src, dst, load_sem.at[k])
+        for k, (src, dst) in enumerate((
+            (hidden_hbm, hidden_ref), (gain_hbm, gain_ref), (freq_hbm, freq_ref),
+            (positions_hbm, positions_ref), (lengths_hbm, lengths_ref),
+            (w_qkv_hbm, w_qkv), (key_hbm, keys), (value_hbm, values), (w_out_hbm, w_out),
+        ))
+    ]
+    for load in loads:
+        load.start()
 
     def swap(src, dst, k):
-        copy = pltpu.make_async_remote_copy(
-            src_ref=src,
-            dst_ref=dst,
-            send_sem=swap_send.at[k],
-            recv_sem=swap_recv.at[k],
-            device_id=partner,
-            device_id_type=MESH,
-        )
-        copy.start()
-        return copy
+        return remote(src, dst, swap_send.at[k], swap_recv.at[k], partner)
 
     sub = sublane()
     upper = sub < 4
     lane = lax.broadcasted_iota(jnp.int32, (8, HEAD), 1)
     token = lax.rem(sub, 4)
-
+    zero = jnp.zeros((8, HEAD), F32)
+
+    loads[0].wait()
     hidden = hidden_ref[...].astype(F32)
     packed = jnp.concatenate([hidden[:, :HEAD], hidden[:, HEAD:]], axis=0).astype(BF16)
-    gain = gain_ref[...].astype(F32)
-    gain2 = jnp.concatenate([gain[:, :HEAD], gain[:, HEAD:]], axis=0).astype(BF16)
     mine1[...] = packed
+    slots1[core, chip] = packed
+    loads[1].wait()
+    gain2 = gain_ref[...].reshape(2, HEAD)
     mineg[...] = gain2
-    slots1[core, chip] = packed
     slotsg[core, chip] = gain2
 
-    loads = [
-        pltpu.make_async_copy(src, dst, load_sem.at[k])
-        for k, (src, dst) in enumerate(
-            ((w_qkv_hbm, w_qkv), (key_hbm, keys), (value_hbm, values), (w_out_hbm, w_out))
-        )
-    ]
-    for load in loads:
-        load.start()
-
-    pl.semaphore_wait(barrier, chips)
-
-    send_all(
-        chips, chip, core,
-        ((lambda _: mine1, slots1.at[core, chip]), (lambda _: mineg, slotsg.at[core, chip])),
-        send_sem.at[0], recv_sem.at[0],
-    )
-
-    position = jnp.zeros((8, HEAD), F32)
+    pl.semaphore_wait(barrier, 2 * reach + 1)
+
+    parts = ((slots1, mine1), (slotsg, mineg))
+
+    def pace(d):
+        return (d - 1) // 2
+
+    for d in range(reach, 0, -1):
+        for side in range(2):
+            for k, (slots, mine) in enumerate(parts):
+                remote(
+                    mine, slots.at[core, chip], send_sem.at[0, k], near_sem.at[side, pace(d), k],
+                    same_core(ahead(d - 2 * d * side), core),
+                )
+
+    loads[2].wait()
+    loads[3].wait()
+    loads[4].wait()
+    position = zero
     for b in range(4):
         position = jnp.where(token == b, positions_ref[b].astype(F32), position)
     angle = position * freq_ref[...]
     cosine = jnp.cos(angle)
     sine = jnp.where(lane < HEAD // 2, -jnp.sin(angle), jnp.sin(angle))
 
-    def rest(slots):
-        return slots.at[0, pl.ds(0, chips - 1)]
-
-    await_bytes(rest(slots1), recv_sem.at[0, 0])
-    await_bytes(rest(slotsg), recv_sem.at[0, 1])
+    def rows_of(slots, count):
+        return slots.at[0, pl.ds(0, count)]
+
+    for step in range(pace(reach) + 1):
+        for side in range(2):
+            for k, (slots, _) in enumerate(parts):
+                await_bytes(rows_of(slots, 2), near_sem.at[side, step, k])
+            for d in (2 * step + 2, 2 * step + 1):
+                if d == reach and side == 1:
+                    continue
+                source = ahead(2 * d * side - d)
+                for k, (slots, _) in enumerate(parts):
+                    block = slots.at[core, source]
+                    remote(
+                        block, block, send_sem.at[0, k], recv_sem.at[0, k],
+                        same_core(ahead(reach - 2 * reach * side), core),
+                    )
+    for k, (slots, _) in enumerate(parts):
+        await_bytes(rows_of(slots, 2 * reach - 1), recv_sem.at[0, k])
     swaps = [swap(slots1.at[core], slots1.at[core], 0), swap(slotsg.at[core], slotsg.at[core], 1)]
 
     def gained(c, s):
@@ -150,7 +160,7 @@
 
         return lax.fori_loop(0, chips, body, carry, unroll=8)
 
-    carry = statistics(core, (jnp.zeros((8, HEAD), F32), jnp.zeros((8, HEAD), F32)))
+    carry = statistics(core, (zero, zero))
     for copy in swaps:
         copy.wait_recv()
     squares, peak = statistics(other, carry)
@@ -164,7 +174,7 @@
     for b in range(4):
         scale_ref[b] = scale[b, 0]
 
-    loads[0].wait()
+    loads[5].wait()
     share = width // (2 * chips)
 
     def project(s, total):
@@ -190,16 +200,31 @@
     piece = jnp.where(upper, turned[:, :HEAD], half_turn(turned[:, HEAD:])).astype(BF16)
     mine2[...] = piece
     slots2[core, chip] = piece
-    send_all(
-        chips, chip, core, ((lambda _: mine2, slots2.at[core, chip]),), send_sem.at[1], recv_sem.at[1]
-    )
-    await_bytes(rest(slots2), recv_sem.at[1, 0])
-    swaps.append(swap(slots2.at[core], slots2.at[core], 2))
-    loads[1].wait()
-    loads[2].wait()
-    swaps[2].wait_recv()
-
-    zero = jnp.zeros((8, HEAD), F32)
+    half = chips // 2
+    far = half - chips // 8
+    own2 = slots2.at[core, chip]
+    for d in range(half, far, -1):
+        for side in range(1 if d == half else 2):
+            target = ahead(d - 2 * d * side)
+            for c in (core, other):
+                remote(mine2, own2, send_sem.at[1, 1], recv_sem.at[1, 1], same_core(target, c))
+    for d in range(far, 0, -1):
+        for side in range(2):
+            remote(
+                mine2, own2, send_sem.at[1, 0], recv_sem.at[1, 0],
+                same_core(ahead(d - 2 * d * side), core),
+            )
+    remote(mine2, own2, swap_send.at[2], swap_recv.at[2], partner)
+    await_bytes(rows_of(slots2, 2 * far), recv_sem.at[1, 0])
+    for d in range(1, far + 1):
+        for side in range(2):
+            block = slots2.at[core, ahead(d - 2 * d * side)]
+            remote(block, block, swap_send.at[2], swap_recv.at[2], partner)
+    loads[6].wait()
+    loads[7].wait()
+    beyond = 2 * (half - far) - 1
+    await_bytes(rows_of(slots2, 2 * beyond), recv_sem.at[1, 1])
+    await_bytes(rows_of(slots2, 2 * far + 1), swap_recv.at[2])
 
     def arrived2(s):
         return slots2[s % 2, s // 2].astype(F32)
@@ -239,10 +264,13 @@
     valid = place < limit
     wide_left = lax.broadcasted_iota(jnp.int32, (rows, HEAD), 1) < HEAD // 2
     even_core = core == 0
-    first_swap = len(swaps)
-    for g in range(KEY_VALUE_HEADS):
-        q = q_bf[rows * g : rows * g + rows, :]
-        heads = slice(HEAD * g, HEAD * g + HEAD)
+    home = me // (QUERY_HEADS // KEY_VALUE_HEADS)
+    order = [lax.rem(home + k, KEY_VALUE_HEADS) for k in (2, 1, 3, 0)]
+
+    def attend(k):
+        g = order[k]
+        q = q_bf[pl.ds(pl.multiple_of(rows * g, rows), rows), :]
+        heads = pl.ds(pl.multiple_of(HEAD * g, HEAD), HEAD)
         scores = jnp.zeros((rows, HEAD), F32)
         for b in range(4):
             part = lax.dot_general(
@@ -260,24 +288,14 @@
             block = jnp.where(row_token == b, part, block)
         stats = jnp.where(wide_left, top, total)
         for j in range(rows // 16):
-            at = 4 * g + j
-            for k, value in enumerate((block, stats)):
+            for i, value in enumerate((block, stats)):
                 one, two = value[16 * j : 16 * j + 8, :], value[16 * j + 8 : 16 * j + 16, :]
                 evens = jnp.where(upper, one, half_turn(two))
                 odds = jnp.where(upper, half_turn(one), two)
-                keep3[at, k] = jnp.where(even_core, evens, odds)
-                give3[at, k] = jnp.where(even_core, odds, evens)
-        part = pl.ds(4 * g, 4)
-        swaps.append(swap(give3.at[part], got3.at[part], 3 + g))
-
-    def pick(ref, start, index):
-        both = ref[pl.ds(pl.multiple_of(start + 8 * (index // 2), 8), 8), :]
-        return jnp.where(lax.rem(index, 2) == 1, half_turn(both), both)
-
-    group = me // (QUERY_HEADS // KEY_VALUE_HEADS)
-    score_new = jnp.sum(pick(q_f32, 0, me) * pick(kv_new, 0, group), axis=1, keepdims=True) * inv
-    score_new = jnp.broadcast_to(score_new, (8, HEAD))
-    value_new = pick(kv_new, 16, group)
+                keep3[4 * k + j, i] = jnp.where(even_core, evens, odds)
+                give3[4 * k + j, i] = jnp.where(even_core, odds, evens)
+        part = pl.ds(4 * k, 4)
+        return swap(give3.at[part], got3.at[part], 3 + k)
 
     left_half = lane < HEAD // 2
 
@@ -285,10 +303,10 @@
         turned = pltpu.roll(value, HEAD // 2, 1)
         return jnp.where(left_half, value, turned), jnp.where(left_half, turned, value)
 
-    for g in range(KEY_VALUE_HEADS):
-        swaps[first_swap + g].wait_recv()
+    def settle(k, copy):
+        copy.wait_recv()
         for j in range(4):
-            at = 4 * g + j
+            at = 4 * k + j
             m0, l0 = both_stats(keep3[at, 1])
             m1, l1 = both_stats(got3[at, 1])
             top = jnp.maximum(m0, m1)
@@ -297,24 +315,50 @@
             block = keep3[at, 0] * f0 + got3[at, 0] * f1
             stats = zero
             for first, left in ((0, top), (3, total)):
-                for k in range(3):
+                for i in range(3):
                     bits = left.astype(BF16).astype(F32)
-                    here = lane >= 16 * (first + k)
-                    stats = jnp.where(here, bits, stats)
+                    stats = jnp.where(lane >= 16 * (first + i), bits, stats)
                     left = left - bits
             stats = jnp.where(lane >= 96, 0.0, stats)
             msg3[2 * at] = jnp.where(upper, block, half_turn(stats)).astype(BF16)
             msg3[2 * at + 1] = jnp.where(upper, half_turn(block), stats).astype(BF16)
-    send_all(
-        chips, chip, core, ((lambda t: msg3.at[t], slots3.at[chip]),), send_sem.at[2], recv_sem.at[2]
-    )
-    slots3[chip] = msg3[chip]
+        for i in range(8):
+            target = 8 * order[k] + i
+
+            def push():
+                remote(
+                    msg3.at[8 * k + i], slots3.at[chip], send_sem.at[2, 0], recv_sem.at[2, 0],
+                    same_core(target, core),
+                )
+
+            if k < 3:
+                push()
+            else:
+                pl.when(target != chip)(push)
+
+    copies = []
+    for k in range(KEY_VALUE_HEADS):
+        copies.append(attend(k))
+        if k >= 2:
+            settle(k - 2, copies[k - 2])
+    settle(2, copies[2])
+    settle(3, copies[3])
+    slots3[chip] = msg3[24 + lax.rem(chip, 8)]
+    swaps.extend(copies)
+
+    def pick(ref, start, index):
+        both = ref[pl.ds(pl.multiple_of(start + 8 * (index // 2), 8), 8), :]
+        return jnp.where(lax.rem(index, 2) == 1, half_turn(both), both)
+
+    score_new = jnp.sum(pick(q_f32, 0, me) * pick(kv_new, 0, home), axis=1, keepdims=True) * inv
+    score_new = jnp.broadcast_to(score_new, (8, HEAD))
+    value_new = pick(kv_new, 16, home)
 
     spot = lax.broadcasted_iota(jnp.int32, (HEAD, 2 * HEAD), 0)
     side = lax.broadcasted_iota(jnp.int32, (HEAD, 2 * HEAD), 1) // HEAD
     chosen = (spot == 48 * side) | (spot == 48 * side + 16) | (spot == 48 * side + 32)
     spread = jnp.where(chosen, 1.0, 0.0).astype(BF16)
-    loads[3].wait()
+    loads[8].wait()
     await_bytes(slots3.at[pl.ds(0, chips - 1)], recv_sem.at[2, 0])
     ml = jnp.dot(slots3[...].reshape(chips * 8, HEAD), spread, preferred_element_type=F32)
     ml = ml.reshape(chips, 8, 2 * HEAD)
@@ -335,29 +379,37 @@
 
     per = w_out.shape[1] // (2 * chips)
 
-    def expand(side, dest):
-        def body(t, _):
-            cols = pl.ds(pl.multiple_of((2 * t + side) * per, per), per)
+    def destination(i):
+        return ahead(half + ((i + 1) // 2) * (1 - 2 * lax.rem(i, 2)))
+
+    batches, batch = 4, chips // 4
+
+    def expand(side, dest, first):
+        for i in range(first, first + batch):
+            cols = pl.ds(pl.multiple_of((2 * destination(i) + side) * per, per), per)
             part = jnp.dot(att, w_out[:, cols], preferred_element_type=F32)
-            dest[t] = jnp.where(upper, part[:, :HEAD], half_turn(part[:, HEAD:]))
-            return 0
-
-        lax.fori_loop(0, chips, body, 0, unroll=8)
-
-    expand(other, give4)
-    last = swap(give4, got4, 3 + KEY_VALUE_HEADS)
-    expand(core, keep4)
-    last.wait_recv()
-
-    def merge(t, _):
-        msg4[t] = (keep4[t] + got4[t]).astype(BF16)
-        return 0
-
-    lax.fori_loop(0, chips, merge, 0, unroll=8)
-    send_all(
-        chips, chip, core, ((lambda t: msg4.at[t], slots4.at[chip]),), send_sem.at[3], recv_sem.at[3]
-    )
-    slots4[chip] = msg4[chip]
+            dest[i] = jnp.where(upper, part[:, :HEAD], half_turn(part[:, HEAD:]))
+
+    copies = []
+    for k in range(batches):
+        expand(other, give4, batch * k)
+        part = pl.ds(batch * k, batch)
+        copies.append(swap(give4.at[part], got4.at[part], 3 + KEY_VALUE_HEADS + k))
+    swaps.extend(copies)
+    for k in range(batches):
+        expand(core, keep4, batch * k)
+    for k in range(batches):
+        copies[k].wait_recv()
+        indices = range(batch * k, batch * k + batch)
+        for i in indices:
+            msg4[i] = (keep4[i] + got4[i]).astype(BF16)
+        for i in indices:
+            if i < chips - 1:
+                remote(
+                    msg4.at[i], slots4.at[chip], send_sem.at[3, 0], recv_sem.at[3, 0],
+                    same_core(destination(i), core),
+                )
+    slots4[chip] = msg4[chips - 1]
     await_bytes(slots4.at[pl.ds(0, chips - 1)], recv_sem.at[3, 0])
 
     def gather_sum(s, total):
@@ -367,12 +419,14 @@
     out_ref[:, :HEAD] = result[0:4, :].astype(BF16)
     out_ref[:, HEAD:] = half_turn(result)[0:4, :].astype(BF16)
 
-    await_bytes(rest(slots1), send_sem.at[0, 0])
-    await_bytes(rest(slotsg), send_sem.at[0, 1])
-    await_bytes(rest(slots2), send_sem.at[1, 0])
+    for k, (slots, _) in enumerate(parts):
+        await_bytes(rows_of(slots, chips - 1), send_sem.at[0, k])
+    await_bytes(rows_of(slots2, 2 * far), send_sem.at[1, 0])
+    await_bytes(rows_of(slots2, 2 * beyond), send_sem.at[1, 1])
+    await_bytes(rows_of(slots2, 2 * far + 1), swap_send.at[2])
     await_bytes(slots3.at[pl.ds(0, chips - 1)], send_sem.at[2, 0])
     await_bytes(slots4.at[pl.ds(0, chips - 1)], send_sem.at[3, 0])
-    for copy in (*swaps, last):
+    for copy in swaps:
         copy.wait_send()
 
 
@@ -394,13 +448,18 @@
             jax.ShapeDtypeStruct(hidden_in.shape, BF16),
             jax.ShapeDtypeStruct((batch,), F32),
         ),
-        in_specs=[smem, smem, vmem, vmem, vmem, anywhere, anywhere, anywhere, anywhere],
+        in_specs=[anywhere] * 9,
         out_specs=(vmem, smem),
         scratch_shapes=[
             pltpu.VMEM(w_qkv.shape[::-1], BF16),
             pltpu.VMEM(w_out.shape, BF16),
             pltpu.VMEM(key_cache.shape, BF16),
             pltpu.VMEM(value_cache.shape, BF16),
+            pltpu.SMEM(lengths.shape, jnp.int32),
+            pltpu.SMEM(positions.shape, jnp.int32),
+            pltpu.VMEM(freq.shape, F32),
+            pltpu.VMEM(hidden_in.shape, BF16),
+            pltpu.VMEM(norm_gain.shape, BF16),
             pltpu.VMEM((8, HEAD), BF16),
             pltpu.VMEM((2, HEAD), BF16),
             pltpu.VMEM((2, chips, 8, HEAD), BF16),
@@ -421,14 +480,15 @@
             tiles_f32,
             tiles,
             tiles,
-            pltpu.SemaphoreType.DMA((4,)),
+            pltpu.SemaphoreType.DMA((9,)),
             pltpu.SemaphoreType.DMA((4, 2)),
+            pltpu.SemaphoreType.DMA((2, chips // 8, 2)),
             pltpu.SemaphoreType.DMA((4, 2)),
-            pltpu.SemaphoreType.DMA((4 + KEY_VALUE_HEADS,)),
-            pltpu.SemaphoreType.DMA((4 + KEY_VALUE_HEADS,)),
+            pltpu.SemaphoreType.DMA((7 + KEY_VALUE_HEADS,)),
+            pltpu.SemaphoreType.DMA((7 + KEY_VALUE_HEADS,)),
         ],
         compiler_params=pltpu.CompilerParams(collective_id=0, has_side_effects=True),
-    )(lengths, positions, freq, hidden_in, norm_gain[None, :], w_qkv.T, w_out, key_cache, value_cache)
+    )(lengths, positions, freq, hidden_in, norm_gain, w_qkv.T, w_out, key_cache, value_cache)
     return attn_out, token_scale
 
 

time: 96.7 us -> 91.6 us (0.947); the launches traced: 95.3 us -> 91.5 us
  Pallas kernels: 91.1 us -> 88.4 us
  local copies, waits for them, and re-layouts: 3.61 us -> 2.39 us
    pallas_call x1, Pallas kernels: 91.1 us -> 88.4 us  [on_device(): pl.pallas_call(functools.partial(kernel, chips), out_shape=(jax.ShapeDtyp...]
    broadcast_in_dim x1 -> x0, local copies, waits for them, and re-layouts: 1.22 us -> none  [on_device(): norm_gain[None, :]]
where the time goes in v3:
time: 91.6 us; the launch traced here: 91.5 us
  Pallas kernels  88.4 us (97%)
  local copies, waits for them, and re-layouts  2.39 us (3%)
    pallas_call x1, Pallas kernels, on_device(): pl.pallas_call(functools.partial(kernel, chips), out_shape=(jax.ShapeDtyp...  88.4 us
    unnamed x2, local copies, waits for them, and re-layouts  2.39 us

profile of v3, /device:TPU:37, one launch (start us, length us, event | category | flops | bytes accessed | tf_op | source)
XLA Modules:
  0.0 91.5 jit_solution(6473158100538925406)
XLA Ops:
  0.6 88.4 %shard_map.104 = (bf16[4,256]{1,0:T(4,128)(2,1)}, f32[4]{0:T(128)}) custom-call(s32[4]{0:T(128)} %lengths_hbm.1, s32[4]{0:T(128)} %positions_hbm.1, f32[1,128]{1,0:T(1,128)} %constant.2.clone.freq_hbm, bf16[4,256]{1,0:T(4,128)(2,1)} %hidden_hbm.1, bf16[256]{0:T(256)(128)(2,1)} %gain_hbm.1, bf16[144,16384]{1,0:T(8,128)(2,1)} %bitcast.1, ...), custom_call_target="tpu_custom_call" | custom-call | tf_op jit(solution)/shard_map/pallas_call | solution.py:445
  89.1 1.3 %copy.13 = bf16[4,256]{1,0:T(4,128)(2,1)} copy(bf16[4,256]{1,0:T(4,128)(2,1)} %get-tuple-element.4) | data formatting | bytes 4096
  90.3 1.1 %copy.14 = f32[4]{0:T(128)} copy(f32[4]{0:T(128)} %get-tuple-element.5) | data formatting | bytes 32

commit v4 on v3

--- a/solution.py
+++ b/solution.py
@@ -50,9 +50,9 @@
     lengths_hbm, positions_hbm, freq_hbm, hidden_hbm, gain_hbm, w_qkv_hbm, w_out_hbm, key_hbm, value_hbm,
     out_ref, scale_ref,
     w_qkv, w_out, keys, values, lengths_ref, positions_ref, freq_ref, hidden_ref, gain_ref,
-    mine1, mineg, slots1, slotsg, proj_ref, mine2, slots2, q_bf, q_f32, kv_new,
+    mine1, mineg, slots1, slotsg, x_ref, proj_ref, mine2, slots2, q_bf, q_f32, kv_new,
     keep3, give3, got3, msg3, slots3, keep4, give4, got4, msg4, slots4,
-    load_sem, send_sem, near_sem, recv_sem, swap_send, swap_recv,
+    load_sem, send_sem, near_sem, cross_sem, recv_sem, swap_send, swap_recv,
 ):
     me = lax.axis_index("tp")
     chip, core = me // 2, lax.rem(me, 2)
@@ -66,9 +66,10 @@
     barrier = pltpu.get_barrier_semaphore()
     for d in range(reach, 0, -1):
         for target in (ahead(d), ahead(-d)):
-            pl.semaphore_signal(
-                barrier, inc=1, device_id=same_core(target, core), device_id_type=MESH
-            )
+            for c in (core, other):
+                pl.semaphore_signal(
+                    barrier, inc=1, device_id=same_core(target, c), device_id_type=MESH
+                )
     pl.semaphore_signal(barrier, inc=1, device_id=partner, device_id_type=MESH)
 
     loads = [
@@ -101,20 +102,31 @@
     mineg[...] = gain2
     slotsg[core, chip] = gain2
 
-    pl.semaphore_wait(barrier, 2 * reach + 1)
-
-    parts = ((slots1, mine1), (slotsg, mineg))
+    pl.semaphore_wait(barrier, 4 * reach + 1)
 
     def pace(d):
         return (d - 1) // 2
 
+    def deliver(hidden, gain, source, target, hidden_sem, gain_sem):
+        peer = same_core(target, core)
+        remote(hidden, slots1.at[core, source], send_sem.at[0, 0], hidden_sem, peer)
+        remote(gain, slotsg.at[core, source], send_sem.at[0, 1], gain_sem, peer)
+        remote(
+            gain, slotsg.at[core, source], send_sem.at[0, 1], cross_sem.at[0], same_core(target, other)
+        )
+
+    def pass_on(source):
+        block = slots1.at[core, source]
+        remote(block, block, swap_send.at[0], swap_recv.at[0], partner)
+
     for d in range(reach, 0, -1):
         for side in range(2):
-            for k, (slots, mine) in enumerate(parts):
-                remote(
-                    mine, slots.at[core, chip], send_sem.at[0, k], near_sem.at[side, pace(d), k],
-                    same_core(ahead(d - 2 * d * side), core),
-                )
+            deliver(
+                mine1, mineg, chip, ahead(d - 2 * d * side),
+                near_sem.at[side, pace(d), 0], near_sem.at[side, pace(d), 1],
+            )
+    remote(mine1, slots1.at[core, chip], swap_send.at[0], swap_recv.at[0], partner)
+    remote(mineg, slotsg.at[core, chip], swap_send.at[1], cross_sem.at[0], partner)
 
     loads[2].wait()
     loads[3].wait()
@@ -129,23 +141,34 @@
     def rows_of(slots, count):
         return slots.at[0, pl.ds(0, count)]
 
-    for step in range(pace(reach) + 1):
+    last_step = pace(reach)
+    for step in range(last_step + 1):
         for side in range(2):
-            for k, (slots, _) in enumerate(parts):
-                await_bytes(rows_of(slots, 2), near_sem.at[side, step, k])
+            await_bytes(rows_of(slots1, 2), near_sem.at[side, step, 0])
+            await_bytes(rows_of(slotsg, 2), near_sem.at[side, step, 1])
             for d in (2 * step + 2, 2 * step + 1):
                 if d == reach and side == 1:
                     continue
                 source = ahead(2 * d * side - d)
-                for k, (slots, _) in enumerate(parts):
-                    block = slots.at[core, source]
-                    remote(
-                        block, block, send_sem.at[0, k], recv_sem.at[0, k],
-                        same_core(ahead(reach - 2 * reach * side), core),
-                    )
-    for k, (slots, _) in enumerate(parts):
-        await_bytes(rows_of(slots, 2 * reach - 1), recv_sem.at[0, k])
-    swaps = [swap(slots1.at[core], slots1.at[core], 0), swap(slotsg.at[core], slotsg.at[core], 1)]
+                target = ahead(reach - 2 * reach * side)
+                arrival = recv_sem.at[0, 0] if step < last_step else cross_sem.at[1]
+                deliver(
+                    slots1.at[core, source], slotsg.at[core, source], source, target,
+                    arrival, recv_sem.at[0, 1],
+                )
+                if step == last_step:
+                    block = slots1.at[core, source]
+                    remote(block, block, send_sem.at[0, 0], cross_sem.at[1], same_core(target, other))
+            for d in (2 * step + 2, 2 * step + 1):
+                pass_on(ahead(2 * d * side - d))
+    relayed = 4 * last_step
+    await_bytes(rows_of(slots1, relayed), recv_sem.at[0, 0])
+    for d in range(1, 2 * last_step + 1):
+        for side in range(2):
+            pass_on(ahead((reach + d) * (2 * side - 1)))
+    await_bytes(rows_of(slots1, 6), cross_sem.at[1])
+    await_bytes(rows_of(slotsg, 2 * reach - 1), recv_sem.at[0, 1])
+    await_bytes(rows_of(slotsg, chips), cross_sem.at[0])
 
     def gained(c, s):
         h = slots1[c, s].astype(F32)
@@ -161,9 +184,10 @@
         return lax.fori_loop(0, chips, body, carry, unroll=8)
 
     carry = statistics(core, (zero, zero))
-    for copy in swaps:
-        copy.wait_recv()
+    passed = 2 * reach + 1 + relayed
+    await_bytes(rows_of(slots1, passed), swap_recv.at[0])
     squares, peak = statistics(other, carry)
+    swaps = []
     squares = squares + half_turn(squares)
     peak = jnp.maximum(peak, half_turn(peak))
     width = w_qkv.shape[1]
@@ -174,22 +198,18 @@
     for b in range(4):
         scale_ref[b] = scale[b, 0]
 
-    loads[5].wait()
     share = width // (2 * chips)
-
-    def project(s, total):
-        for c in range(2):
+    for c in range(2):
+        for s in range(chips):
             _, hg = gained(c, s)
             quant = (hg * rstd) / scale
-            x = jnp.concatenate([quant, half_turn(quant)], axis=1).astype(BF16)
-            rows = pl.ds(pl.multiple_of((2 * s + c) * share, share), share)
-            total = total + lax.dot_general(
-                x, w_qkv[:, rows], (((1,), (1,)), ((), ())), preferred_element_type=F32
-            )
-        return total
-
+            at = (2 * s + c) * share
+            x_ref[:, at : at + share] = jnp.concatenate([quant, half_turn(quant)], axis=1).astype(BF16)
+    loads[5].wait()
     columns = w_qkv.shape[0]
-    proj = lax.fori_loop(0, chips, project, jnp.zeros((8, columns), F32), unroll=8)
+    proj = lax.dot_general(
+        x_ref[...], w_qkv[...], (((1,), (1,)), ((), ())), preferred_element_type=F32
+    )
     proj_ref[...] = jnp.zeros((8, 2 * HEAD), F32)
     proj_ref[:, :columns] = proj * scale[:, 0:1]
     wide = proj_ref[...]
@@ -383,6 +403,7 @@
         return ahead(half + ((i + 1) // 2) * (1 - 2 * lax.rem(i, 2)))
 
     batches, batch = 4, chips // 4
+    early = batch
 
     def expand(side, dest, first):
         for i in range(first, first + batch):
@@ -406,21 +427,25 @@
         for i in indices:
             if i < chips - 1:
                 remote(
-                    msg4.at[i], slots4.at[chip], send_sem.at[3, 0], recv_sem.at[3, 0],
+                    msg4.at[i], slots4.at[i], send_sem.at[3, 0], recv_sem.at[3, int(i >= early)],
                     same_core(destination(i), core),
                 )
-    slots4[chip] = msg4[chips - 1]
-    await_bytes(slots4.at[pl.ds(0, chips - 1)], recv_sem.at[3, 0])
-
-    def gather_sum(s, total):
-        return total + slots4[s].astype(F32)
-
-    result = lax.fori_loop(0, chips, gather_sum, zero, unroll=8)
+    slots4[chips - 1] = msg4[chips - 1]
+    await_bytes(slots4.at[pl.ds(0, chips - 1 - early)], recv_sem.at[3, 1])
+    sums = [zero] * 4
+    for i in range(chips - 1, early - 1, -1):
+        sums[i % 4] = sums[i % 4] + slots4[i].astype(F32)
+    await_bytes(slots4.at[pl.ds(0, early)], recv_sem.at[3, 0])
+    for i in range(early):
+        sums[i % 4] = sums[i % 4] + slots4[i].astype(F32)
+    result = (sums[0] + sums[1]) + (sums[2] + sums[3])
     out_ref[:, :HEAD] = result[0:4, :].astype(BF16)
     out_ref[:, HEAD:] = half_turn(result)[0:4, :].astype(BF16)
 
-    for k, (slots, _) in enumerate(parts):
-        await_bytes(rows_of(slots, chips - 1), send_sem.at[0, k])
+    await_bytes(slots1.at[:, pl.ds(0, 2 * reach + 1)], send_sem.at[0, 0])
+    await_bytes(slotsg.at[:, pl.ds(0, chips - 1)], send_sem.at[0, 1])
+    await_bytes(mineg, swap_send.at[1])
+    await_bytes(rows_of(slots1, passed), swap_send.at[0])
     await_bytes(rows_of(slots2, 2 * far), send_sem.at[1, 0])
     await_bytes(rows_of(slots2, 2 * beyond), send_sem.at[1, 1])
     await_bytes(rows_of(slots2, 2 * far + 1), swap_send.at[2])
@@ -464,6 +489,7 @@
             pltpu.VMEM((2, HEAD), BF16),
             pltpu.VMEM((2, chips, 8, HEAD), BF16),
             pltpu.VMEM((2, chips, 2, HEAD), BF16),
+            pltpu.VMEM((8, w_qkv.shape[0]), BF16),
             pltpu.VMEM((8, 2 * HEAD), F32),
             pltpu.VMEM((8, HEAD), BF16),
             pltpu.VMEM((2, chips, 8, HEAD), BF16),
@@ -483,6 +509,7 @@
             pltpu.SemaphoreType.DMA((9,)),
             pltpu.SemaphoreType.DMA((4, 2)),
             pltpu.SemaphoreType.DMA((2, chips // 8, 2)),
+            pltpu.SemaphoreType.DMA((2,)),
             pltpu.SemaphoreType.DMA((4, 2)),
             pltpu.SemaphoreType.DMA((7 + KEY_VALUE_HEADS,)),
             pltpu.SemaphoreType.DMA((7 + KEY_VALUE_HEADS,)),

time: 91.6 us -> 94.3 us (1.029)
  Pallas kernels: 88.4 us -> 91.1 us
    pallas_call x1, Pallas kernels: 88.4 us -> 91.1 us  [on_device(): pl.pallas_call(functools.partial(kernel, chips), out_shape=(jax.ShapeDtyp...]
where the time goes in v4:
time: 94.3 us; the launch traced here: 94.1 us
  Pallas kernels  91.1 us (97%)
  local copies, waits for them, and re-layouts  2.39 us (3%)
    pallas_call x1, Pallas kernels, on_device(): pl.pallas_call(functools.partial(kernel, chips), out_shape=(jax.ShapeDtyp...  91.1 us
    unnamed x2, local copies, waits for them, and re-layouts  2.39 us

profile of v4, /device:TPU:37, one launch (start us, length us, event | category | flops | bytes accessed | tf_op | source)
XLA Modules:
  0.0 94.1 jit_solution(12638792263493991137)
XLA Ops:
  0.6 91.1 %shard_map.104 = (bf16[4,256]{1,0:T(4,128)(2,1)}, f32[4]{0:T(128)}) custom-call(s32[4]{0:T(128)} %lengths_hbm.1, s32[4]{0:T(128)} %positions_hbm.1, f32[1,128]{1,0:T(1,128)} %constant.2.clone.freq_hbm, bf16[4,256]{1,0:T(4,128)(2,1)} %hidden_hbm.1, bf16[256]{0:T(256)(128)(2,1)} %gain_hbm.1, bf16[144,16384]{1,0:T(8,128)(2,1)} %bitcast.1, ...), custom_call_target="tpu_custom_call" | custom-call | tf_op jit(solution)/shard_map/pallas_call | solution.py:470
  91.7 1.3 %copy.13 = bf16[4,256]{1,0:T(4,128)(2,1)} copy(bf16[4,256]{1,0:T(4,128)(2,1)} %get-tuple-element.4) | data formatting | bytes 4096
  93.0 1.1 %copy.14 = f32[4]{0:T(128)} copy(f32[4]{0:T(128)} %get-tuple-element.5) | data formatting | bytes 32

commit v5 on v3

--- a/solution.py
+++ b/solution.py
@@ -171,8 +171,7 @@
     peak = jnp.broadcast_to(jnp.max(peak, axis=1, keepdims=True), (8, HEAD))
     rstd = lax.rsqrt(squares / width + 1e-05)
     scale = (peak * rstd + 1e-06) / 448.0
-    for b in range(4):
-        scale_ref[b] = scale[b, 0]
+    scale_ref[...] = scale
 
     loads[5].wait()
     share = width // (2 * chips)
@@ -201,30 +200,15 @@
     mine2[...] = piece
     slots2[core, chip] = piece
     half = chips // 2
-    far = half - chips // 8
     own2 = slots2.at[core, chip]
-    for d in range(half, far, -1):
+    for d in range(half, 0, -1):
         for side in range(1 if d == half else 2):
-            target = ahead(d - 2 * d * side)
-            for c in (core, other):
-                remote(mine2, own2, send_sem.at[1, 1], recv_sem.at[1, 1], same_core(target, c))
-    for d in range(far, 0, -1):
-        for side in range(2):
-            remote(
-                mine2, own2, send_sem.at[1, 0], recv_sem.at[1, 0],
-                same_core(ahead(d - 2 * d * side), core),
-            )
-    remote(mine2, own2, swap_send.at[2], swap_recv.at[2], partner)
-    await_bytes(rows_of(slots2, 2 * far), recv_sem.at[1, 0])
-    for d in range(1, far + 1):
-        for side in range(2):
-            block = slots2.at[core, ahead(d - 2 * d * side)]
-            remote(block, block, swap_send.at[2], swap_recv.at[2], partner)
+            remote(mine2, own2, send_sem.at[1, 0], recv_sem.at[1, 0], same_core(ahead(d - 2 * d * side), core))
+    await_bytes(rows_of(slots2, chips - 1), recv_sem.at[1, 0])
+    swaps.append(swap(slots2.at[core], slots2.at[core], 2))
     loads[6].wait()
     loads[7].wait()
-    beyond = 2 * (half - far) - 1
-    await_bytes(rows_of(slots2, 2 * beyond), recv_sem.at[1, 1])
-    await_bytes(rows_of(slots2, 2 * far + 1), swap_recv.at[2])
+    await_bytes(slots2.at[0], swap_recv.at[2])
 
     def arrived2(s):
         return slots2[s % 2, s // 2].astype(F32)
@@ -421,9 +405,7 @@
 
     for k, (slots, _) in enumerate(parts):
         await_bytes(rows_of(slots, chips - 1), send_sem.at[0, k])
-    await_bytes(rows_of(slots2, 2 * far), send_sem.at[1, 0])
-    await_bytes(rows_of(slots2, 2 * beyond), send_sem.at[1, 1])
-    await_bytes(rows_of(slots2, 2 * far + 1), swap_send.at[2])
+    await_bytes(rows_of(slots2, chips - 1), send_sem.at[1, 0])
     await_bytes(slots3.at[pl.ds(0, chips - 1)], send_sem.at[2, 0])
     await_bytes(slots4.at[pl.ds(0, chips - 1)], send_sem.at[3, 0])
     for copy in swaps:
@@ -445,11 +427,11 @@
     attn_out, token_scale = pl.pallas_call(
         functools.partial(kernel, chips),
         out_shape=(
-            jax.ShapeDtypeStruct(hidden_in.shape, BF16),
-            jax.ShapeDtypeStruct((batch,), F32),
+            pltpu.VMEM(hidden_in.shape, BF16),
+            pltpu.VMEM((8, HEAD), F32),
         ),
         in_specs=[anywhere] * 9,
-        out_specs=(vmem, smem),
+        out_specs=(vmem, vmem),
         scratch_shapes=[
             pltpu.VMEM(w_qkv.shape[::-1], BF16),
             pltpu.VMEM(w_out.shape, BF16),
@@ -489,7 +471,7 @@
         ],
         compiler_params=pltpu.CompilerParams(collective_id=0, has_side_effects=True),
     )(lengths, positions, freq, hidden_in, norm_gain, w_qkv.T, w_out, key_cache, value_cache)
-    return attn_out, token_scale
+    return attn_out, token_scale[:batch, 0]
 
 
 def solution(mesh):

time: 91.6 us -> 87.2 us (0.952)
  Pallas kernels: 88.4 us -> 85.2 us
  local copies, waits for them, and re-layouts: 2.39 us -> 1.21 us
    pallas_call x1, Pallas kernels: 88.4 us -> 85.2 us  [on_device(): pl.pallas_call(functools.partial(kernel, chips), out_shape=(pltpu.VMEM(hi...]
    unnamed x2 -> x1, local copies, waits for them, and re-layouts: 2.39 us -> 0.58 us
where the time goes in v5:
time: 87.2 us; the launch traced here: 87.1 us
  Pallas kernels  85.2 us (98%)
  local copies, waits for them, and re-layouts  1.21 us (1%)
    pallas_call x1, Pallas kernels, on_device(): pl.pallas_call(functools.partial(kernel, chips), out_shape=(pltpu.VMEM(hi...  85.2 us

profile of v5, /device:TPU:37, one launch (start us, length us, event | category | flops | bytes accessed | tf_op | source)
XLA Modules:
  0.0 87.1 jit_solution(15594599017422123595)
XLA Ops:
  0.6 85.2 %shard_map.104 = (bf16[4,256]{1,0:T(4,128)(2,1)S(1)}, f32[8,128]{1,0:T(8,128)S(1)}) custom-call(s32[4]{0:T(128)} %lengths_hbm.1, s32[4]{0:T(128)} %positions_hbm.1, f32[1,128]{1,0:T(1,128)} %constant.2.clone.freq_hbm, bf16[4,256]{1,0:T(4,128)(2,1)} %hidden_hbm.1, bf16[256]{0:T(256)(128)(2,1)} %gain_hbm.1, bf16[144,16384]{1,0:T(8,128)(2,1)} %bitcast.1, ...), custom_call_target="tpu_custom_call" | custom-call | tf_op jit(solution)/shard_map/pallas_call | solution.py:427
  85.9 0.6 copy.12
  86.5 0.6 slice_reduce_fusion

commit v6 on v5

--- a/solution.py
+++ b/solution.py
@@ -50,8 +50,8 @@
     lengths_hbm, positions_hbm, freq_hbm, hidden_hbm, gain_hbm, w_qkv_hbm, w_out_hbm, key_hbm, value_hbm,
     out_ref, scale_ref,
     w_qkv, w_out, keys, values, lengths_ref, positions_ref, freq_ref, hidden_ref, gain_ref,
-    mine1, mineg, slots1, slotsg, proj_ref, mine2, slots2, q_bf, q_f32, kv_new,
-    keep3, give3, got3, msg3, slots3, keep4, give4, got4, msg4, slots4,
+    mine1, mineg, slots1, slotsg, proj_ref, mine2, slots2, q_bf, q_f32,
+    msg3, slots3, keep4, give4, got4, msg4, slots4,
     load_sem, send_sem, near_sem, recv_sem, swap_send, swap_recv,
 ):
     me = lax.axis_index("tp")
@@ -76,7 +76,7 @@
         for k, (src, dst) in enumerate((
             (hidden_hbm, hidden_ref), (gain_hbm, gain_ref), (freq_hbm, freq_ref),
             (positions_hbm, positions_ref), (lengths_hbm, lengths_ref),
-            (w_qkv_hbm, w_qkv), (key_hbm, keys), (value_hbm, values), (w_out_hbm, w_out),
+            (w_qkv_hbm, w_qkv), (key_hbm, keys.at[core]), (value_hbm, values.at[core]), (w_out_hbm, w_out),
         ))
     ]
     for load in loads:
@@ -196,118 +196,133 @@
     turned = wide
     for k in range(1, 8):
         turned = jnp.where(turn == k, pltpu.roll(wide, 16 * k, 1), turned)
-    piece = jnp.where(upper, turned[:, :HEAD], half_turn(turned[:, HEAD:])).astype(BF16)
-    mine2[...] = piece
-    slots2[core, chip] = piece
+    mine2[0] = turned[0:4, :HEAD].astype(BF16)
+    mine2[1] = turned[0:4, HEAD:].astype(BF16)
+
     half = chips // 2
-    own2 = slots2.at[core, chip]
+    home = chip // 8
+    first = me + me // 8
+    seam = QUERY_HEADS - QUERY_HEADS // 8
+
+    def part_for(target, c):
+        by_core = lax.rem(first + c, 2)
+        by_group = jnp.where(target // 8 == lax.rem(me - seam + 3, 4), 0, 1)
+        return mine2.at[jnp.where(me > seam, by_group, by_core)]
+
+    def send2(d, c):
+        target = ahead(d)
+        remote(
+            part_for(target, c), slots2.at[me], send_sem.at[1, 0],
+            recv_sem.at[1, int(abs(d) <= 4)], same_core(target, c),
+        )
+
     for d in range(half, 0, -1):
-        for side in range(1 if d == half else 2):
-            remote(mine2, own2, send_sem.at[1, 0], recv_sem.at[1, 0], same_core(ahead(d - 2 * d * side), core))
-    await_bytes(rows_of(slots2, chips - 1), recv_sem.at[1, 0])
-    swaps.append(swap(slots2.at[core], slots2.at[core], 2))
+        for c in range(2):
+            send2(d, c)
+            if d < half:
+                send2(-d, c)
+    remote(part_for(chip, other), slots2.at[me], send_sem.at[1, 0], recv_sem.at[1, 1], partner)
+
+    @pl.when(me == seam)
+    def _():
+        for target in range(8):
+            for c in range(2):
+                remote(
+                    mine2.at[1], slots2.at[2 * chips], send_sem.at[1, 1], recv_sem.at[2, 1],
+                    same_core(target, c),
+                )
+
+    none = 2 * chips + 1
+    slots2[me] = part_for(chip, core)[...]
+    slots2[none] = jnp.zeros((4, HEAD), BF16)
     loads[6].wait()
     loads[7].wait()
-    await_bytes(slots2.at[0], swap_recv.at[2])
-
-    def arrived2(s):
-        return slots2[s % 2, s // 2].astype(F32)
-
-    def halves(h):
+    await_bytes(slots2.at[pl.ds(0, 17)], recv_sem.at[1, 1])
+    swaps.append(swap(keys.at[core], keys.at[core], 2))
+    swaps.append(swap(values.at[core], values.at[core], 3))
+    await_bytes(slots2.at[pl.ds(0, 2 * chips - 18)], recv_sem.at[1, 0])
+
+    @pl.when(home == 0)
+    def _():
+        await_bytes(slots2.at[pl.ds(0, 1)], recv_sem.at[2, 1])
+
+    def sources(h):
         g, k = h // 9, h % 9
-        first = arrived2(8 * g + k) if k < 8 else None
-        second = arrived2(8 * g + k - 1) if k > 0 else None
-        return first, second
-
-    def pair(p):
-        a0, b0 = halves(2 * p)
-        a1, b1 = halves(2 * p + 1)
-        low = (a0 if a0 is not None else zero) + (half_turn(b0) if b0 is not None else zero)
-        high = (half_turn(a1) if a1 is not None else zero) + (b1 if b1 is not None else zero)
-        return jnp.where(upper, low, high)
+        return 8 * g + k if k < 8 else none, 8 * g + k - 1 if k > 0 else none
+
+    def joined(a, b):
+        return slots2[a].astype(F32) + slots2[b].astype(F32)
+
+    def own_head(i):
+        even, odd = sources(2 * i), sources(2 * i + 1)
+        return joined(*(e + core * (o - e) for e, o in zip(even, odd)))
 
     def rotated(value):
-        return value * cosine + pltpu.roll(value, HEAD // 2, 1) * sine
-
-    for p in range(QUERY_HEADS // 2):
-        q = rotated(pair(p)).astype(BF16)
+        count = value.shape[0]
+        return value * cosine[:count] + pltpu.roll(value, HEAD // 2, 1) * sine[:count]
+
+    for p in range(chips // 2):
+        q = rotated(jnp.concatenate([own_head(2 * p), own_head(2 * p + 1)], axis=0)).astype(BF16)
         q_bf[8 * p : 8 * p + 8, :] = q
         q_f32[8 * p : 8 * p + 8, :] = q.astype(F32)
-    base = QUERY_HEADS // 2
-    for p in range(2):
-        kv_new[8 * p : 8 * p + 8, :] = rotated(pair(base + p))
-        kv_new[16 + 8 * p : 24 + 8 * p, :] = pair(base + 2 + p)
+    key_new = joined(seam + 1 + home, jnp.where(home == 0, 2 * chips, seam + home))
+    key_new = rotated(jnp.concatenate([key_new, key_new], axis=0))
+    value_new = joined(jnp.where(home == 3, none, seam + 5 + home), seam + 4 + home)
+    value_new = jnp.concatenate([value_new, value_new], axis=0)
 
     inv = 1.0 / HEAD**0.5
-    rows = 64
+    rows = 32
     row_token = lax.rem(lax.broadcasted_iota(jnp.int32, (rows, HEAD), 0), 4)
-    place = me * keys.shape[1] + lax.broadcasted_iota(jnp.int32, (rows, HEAD), 1)
+    wide_lane = lax.broadcasted_iota(jnp.int32, (rows, HEAD), 1)
     limit = jnp.zeros((rows, HEAD), jnp.int32)
     for b in range(4):
         limit = jnp.where(row_token == b, lengths_ref[b], limit)
-    valid = place < limit
-    wide_left = lax.broadcasted_iota(jnp.int32, (rows, HEAD), 1) < HEAD // 2
-    even_core = core == 0
-    home = me // (QUERY_HEADS // KEY_VALUE_HEADS)
+    span = keys.shape[2]
     order = [lax.rem(home + k, KEY_VALUE_HEADS) for k in (2, 1, 3, 0)]
+    for copy in swaps[2:4]:
+        copy.wait_recv()
 
     def attend(k):
         g = order[k]
         q = q_bf[pl.ds(pl.multiple_of(rows * g, rows), rows), :]
         heads = pl.ds(pl.multiple_of(HEAD * g, HEAD), HEAD)
-        scores = jnp.zeros((rows, HEAD), F32)
-        for b in range(4):
-            part = lax.dot_general(
-                q, keys[b, :, heads], (((1,), (1,)), ((), ())), preferred_element_type=F32
-            )
-            scores = jnp.where(row_token == b, part, scores)
-        scores = scores * inv
-        top = jnp.max(jnp.where(valid, scores, -1e30), axis=1, keepdims=True)
-        weights = jnp.where(valid, jnp.exp(scores - top), 0.0)
-        total = jnp.sum(weights, axis=1, keepdims=True)
-        rounded = weights.astype(BF16)
-        block = jnp.zeros((rows, HEAD), F32)
-        for b in range(4):
-            part = jnp.dot(rounded, values[b, :, heads], preferred_element_type=F32)
-            block = jnp.where(row_token == b, part, block)
-        stats = jnp.where(wide_left, top, total)
-        for j in range(rows // 16):
-            for i, value in enumerate((block, stats)):
-                one, two = value[16 * j : 16 * j + 8, :], value[16 * j + 8 : 16 * j + 16, :]
-                evens = jnp.where(upper, one, half_turn(two))
-                odds = jnp.where(upper, half_turn(one), two)
-                keep3[4 * k + j, i] = jnp.where(even_core, evens, odds)
-                give3[4 * k + j, i] = jnp.where(even_core, odds, evens)
-        part = pl.ds(4 * k, 4)
-        return swap(give3.at[part], got3.at[part], 3 + k)
-
-    left_half = lane < HEAD // 2
-
-    def both_stats(value):
-        turned = pltpu.roll(value, HEAD // 2, 1)
-        return jnp.where(left_half, value, turned), jnp.where(left_half, turned, value)
-
-    def settle(k, copy):
-        copy.wait_recv()
-        for j in range(4):
-            at = 4 * k + j
-            m0, l0 = both_stats(keep3[at, 1])
-            m1, l1 = both_stats(got3[at, 1])
-            top = jnp.maximum(m0, m1)
-            f0, f1 = jnp.exp(m0 - top), jnp.exp(m1 - top)
-            total = l0 * f0 + l1 * f1
-            block = keep3[at, 0] * f0 + got3[at, 0] * f1
-            stats = zero
-            for first, left in ((0, top), (3, total)):
-                for i in range(3):
-                    bits = left.astype(BF16).astype(F32)
-                    stats = jnp.where(lane >= 16 * (first + i), bits, stats)
-                    left = left - bits
-            stats = jnp.where(lane >= 96, 0.0, stats)
-            msg3[2 * at] = jnp.where(upper, block, half_turn(stats)).astype(BF16)
-            msg3[2 * at + 1] = jnp.where(upper, half_turn(block), stats).astype(BF16)
+        found = []
+        for c in range(2):
+            scores = jnp.zeros((rows, HEAD), F32)
+            for b in range(4):
+                part = lax.dot_general(
+                    q, keys[c, b, :, heads], (((1,), (1,)), ((), ())), preferred_element_type=F32
+                )
+                scores = jnp.where(row_token == b, part, scores)
+            scores = scores * inv
+            valid = (2 * chip + c) * span + wide_lane < limit
+            top = jnp.max(jnp.where(valid, scores, -1e30), axis=1, keepdims=True)
+            weights = jnp.where(valid, jnp.exp(scores - top), 0.0)
+            total = jnp.sum(weights, axis=1, keepdims=True)
+            rounded = weights.astype(BF16)
+            block = jnp.zeros((rows, HEAD), F32)
+            for b in range(4):
+                part = jnp.dot(rounded, values[c, b, :, heads], preferred_element_type=F32)
+                block = jnp.where(row_token == b, part, block)
+            found.append((top, total, block))
+        (m0, l0, o0), (m1, l1, o1) = found
+        top = jnp.maximum(m0, m1)
+        f0, f1 = jnp.exp(m0 - top), jnp.exp(m1 - top)
+        total = l0 * f0 + l1 * f1
+        block = o0 * f0 + o1 * f1
+        stats = jnp.zeros((rows, HEAD), F32)
+        for at, left in ((0, top), (3, total)):
+            for i in range(3):
+                bits = left.astype(BF16).astype(F32)
+                stats = jnp.where(wide_lane >= 16 * (at + i), bits, stats)
+                left = left - bits
+        stats = jnp.where(wide_lane >= 96, 0.0, stats)
+        for j in range(rows // 8):
+            o, t = block[8 * j : 8 * j + 8, :], stats[8 * j : 8 * j + 8, :]
+            msg3[8 * k + 2 * j] = jnp.where(upper, o, half_turn(t)).astype(BF16)
+            msg3[8 * k + 2 * j + 1] = jnp.where(upper, half_turn(o), t).astype(BF16)
         for i in range(8):
-            target = 8 * order[k] + i
+            target = 8 * g + i
 
             def push():
                 remote(
@@ -320,23 +335,14 @@
             else:
                 pl.when(target != chip)(push)
 
-    copies = []
     for k in range(KEY_VALUE_HEADS):
-        copies.append(attend(k))
-        if k >= 2:
-            settle(k - 2, copies[k - 2])
-    settle(2, copies[2])
-    settle(3, copies[3])
+        attend(k)
     slots3[chip] = msg3[24 + lax.rem(chip, 8)]
-    swaps.extend(copies)
-
-    def pick(ref, start, index):
-        both = ref[pl.ds(pl.multiple_of(start + 8 * (index // 2), 8), 8), :]
-        return jnp.where(lax.rem(index, 2) == 1, half_turn(both), both)
-
-    score_new = jnp.sum(pick(q_f32, 0, me) * pick(kv_new, 0, home), axis=1, keepdims=True) * inv
+
+    both = q_f32[pl.ds(pl.multiple_of(8 * (chip // 2), 8), 8), :]
+    own_q = jnp.where(lax.rem(chip, 2) == 1, half_turn(both), both)
+    score_new = jnp.sum(own_q * key_new, axis=1, keepdims=True) * inv
     score_new = jnp.broadcast_to(score_new, (8, HEAD))
-    value_new = pick(kv_new, 16, home)
 
     spot = lax.broadcasted_iota(jnp.int32, (HEAD, 2 * HEAD), 0)
     side = lax.broadcasted_iota(jnp.int32, (HEAD, 2 * HEAD), 1) // HEAD
@@ -366,35 +372,59 @@
     def destination(i):
         return ahead(half + ((i + 1) // 2) * (1 - 2 * lax.rem(i, 2)))
 
-    batches, batch = 4, chips // 4
-
-    def expand(side, dest, first):
+    batches, batch = 4, chips // 8
+
+    def expand(offset, dest, first):
         for i in range(first, first + batch):
-            cols = pl.ds(pl.multiple_of((2 * destination(i) + side) * per, per), per)
+            target = destination(offset + i)
+            cols = pl.ds(pl.multiple_of(2 * per * target, 2 * per), 2 * per)
             part = jnp.dot(att, w_out[:, cols], preferred_element_type=F32)
-            dest[i] = jnp.where(upper, part[:, :HEAD], half_turn(part[:, HEAD:]))
+            for c in range(2):
+                low = part[:, per * c : per * c + HEAD]
+                high = part[:, per * c + HEAD : per * c + per]
+                dest[2 * i + c] = jnp.where(upper, low, half_turn(high))
 
     copies = []
     for k in range(batches):
-        expand(other, give4, batch * k)
-        part = pl.ds(batch * k, batch)
-        copies.append(swap(give4.at[part], got4.at[part], 3 + KEY_VALUE_HEADS + k))
+        expand(half * core, give4, batch * k)
+        part = pl.ds(2 * batch * k, 2 * batch)
+        copies.append(swap(give4.at[part], got4.at[part], 4 + k))
     swaps.extend(copies)
     for k in range(batches):
-        expand(core, keep4, batch * k)
+        expand(half * other, keep4, batch * k)
     for k in range(batches):
         copies[k].wait_recv()
-        indices = range(batch * k, batch * k + batch)
+        indices = range(2 * batch * k, 2 * batch * k + 2 * batch)
         for i in indices:
             msg4[i] = (keep4[i] + got4[i]).astype(BF16)
         for i in indices:
-            if i < chips - 1:
+            place = half * other + i // 2
+            if i // 2 < half - 1:
                 remote(
-                    msg4.at[i], slots4.at[chip], send_sem.at[3, 0], recv_sem.at[3, 0],
-                    same_core(destination(i), core),
+                    msg4.at[i], slots4.at[place], send_sem.at[3, 0], recv_sem.at[3, 0],
+                    same_core(destination(place), i % 2),
                 )
-    slots4[chip] = msg4[chips - 1]
+
+    @pl.when(core == 1)
+    def _():
+        for i in (chips - 2, chips - 1):
+            remote(
+                msg4.at[i], slots4.at[half - 1], send_sem.at[3, 1], recv_sem.at[3, 0],
+                same_core(destination(half - 1), i % 2),
+            )
+
+    @pl.when(core == 0)
+    def _():
+        remote(
+            msg4.at[chips - 1], slots4.at[chips - 1], send_sem.at[3, 1], recv_sem.at[3, 1], partner
+        )
+        slots4[chips - 1] = msg4[chips - 2]
+
     await_bytes(slots4.at[pl.ds(0, chips - 1)], recv_sem.at[3, 0])
+
+    @pl.when(core == 1)
+    def _():
+        await_bytes(slots4.at[pl.ds(0, 1)], recv_sem.at[3, 1])
 
     def gather_sum(s, total):
         return total + slots4[s].astype(F32)
@@ -405,9 +435,23 @@
 
     for k, (slots, _) in enumerate(parts):
         await_bytes(rows_of(slots, chips - 1), send_sem.at[0, k])
-    await_bytes(rows_of(slots2, chips - 1), send_sem.at[1, 0])
+    await_bytes(slots2.at[pl.ds(0, 2 * chips - 1)], send_sem.at[1, 0])
+
+    @pl.when(me == seam)
+    def _():
+        await_bytes(slots2.at[pl.ds(0, 16)], send_sem.at[1, 1])
+
     await_bytes(slots3.at[pl.ds(0, chips - 1)], send_sem.at[2, 0])
-    await_bytes(slots4.at[pl.ds(0, chips - 1)], send_sem.at[3, 0])
+    await_bytes(slots4.at[pl.ds(0, chips - 2)], send_sem.at[3, 0])
+
+    @pl.when(core == 1)
+    def _():
+        await_bytes(slots4.at[pl.ds(0, 2)], send_sem.at[3, 1])
+
+    @pl.when(core == 0)
+    def _():
+        await_bytes(slots4.at[pl.ds(0, 1)], send_sem.at[3, 1])
+
     for copy in swaps:
         copy.wait_send()
 
@@ -423,7 +467,6 @@
     batch = hidden_in.shape[0]
     tiles = pltpu.VMEM((chips, 8, HEAD), BF16)
     tiles_f32 = pltpu.VMEM((chips, 8, HEAD), F32)
-    stats = pltpu.VMEM((chips // 2, 2, 8, HEAD), F32)
     attn_out, token_scale = pl.pallas_call(
         functools.partial(kernel, chips),
         out_shape=(
@@ -435,8 +478,8 @@
         scratch_shapes=[
             pltpu.VMEM(w_qkv.shape[::-1], BF16),
             pltpu.VMEM(w_out.shape, BF16),
-            pltpu.VMEM(key_cache.shape, BF16),
-            pltpu.VMEM(value_cache.shape, BF16),
+            pltpu.VMEM((2, *key_cache.shape), BF16),
+            pltpu.VMEM((2, *value_cache.shape), BF16),
             pltpu.SMEM(lengths.shape, jnp.int32),
             pltpu.SMEM(positions.shape, jnp.int32),
             pltpu.VMEM(freq.shape, F32),
@@ -447,14 +490,10 @@
             pltpu.VMEM((2, chips, 8, HEAD), BF16),
             pltpu.VMEM((2, chips, 2, HEAD), BF16),
             pltpu.VMEM((8, 2 * HEAD), F32),
-            pltpu.VMEM((8, HEAD), BF16),
-            pltpu.VMEM((2, chips, 8, HEAD), BF16),
-            pltpu.VMEM((4 * QUERY_HEADS, HEAD), BF16),
-            pltpu.VMEM((4 * QUERY_HEADS, HEAD), F32),
-            pltpu.VMEM((32, HEAD), F32),
-            stats,
-            stats,
-            stats,
+            pltpu.VMEM((2, 4, HEAD), BF16),
+            pltpu.VMEM((2 * chips + 2, 4, HEAD), BF16),
+            pltpu.VMEM((2 * QUERY_HEADS, HEAD), BF16),
+            pltpu.VMEM((2 * QUERY_HEADS, HEAD), F32),
             tiles,
             tiles,
             tiles_f32,

time: 87.2 us -> 86 us (0.986)
  Pallas kernels: 85.2 us -> 84.1 us
    pallas_call x1, Pallas kernels: 85.2 us -> 84.1 us  [on_device(): pl.pallas_call(functools.partial(kernel, chips), out_shape=(pltpu.VMEM(hi...]
where the time goes in v6:
time: 86 us; the launch traced here: 85.9 us
  Pallas kernels  84.1 us (98%)
  local copies, waits for them, and re-layouts  1.21 us (1%)
    pallas_call x1, Pallas kernels, on_device(): pl.pallas_call(functools.partial(kernel, chips), out_shape=(pltpu.VMEM(hi...  84.1 us

profile of v6, /device:TPU:37, one launch (start us, length us, event | category | flops | bytes accessed | tf_op | source)
XLA Modules:
  0.0 85.9 jit_solution(9459000484037010409)
XLA Ops:
  0.6 84.1 %shard_map.104 = (bf16[4,256]{1,0:T(4,128)(2,1)S(1)}, f32[8,128]{1,0:T(8,128)S(1)}) custom-call(s32[4]{0:T(128)} %lengths_hbm.1, s32[4]{0:T(128)} %positions_hbm.1, f32[1,128]{1,0:T(1,128)} %constant.2.clone.freq_hbm, bf16[4,256]{1,0:T(4,128)(2,1)} %hidden_hbm.1, bf16[256]{0:T(256)(128)(2,1)} %gain_hbm.1, bf16[144,16384]{1,0:T(8,128)(2,1)} %bitcast.1, ...), custom_call_target="tpu_custom_call" | custom-call | tf_op jit(solution)/shard_map/pallas_call | solution.py:470
  84.7 0.6 copy.12
  85.3 0.6 slice_reduce_fusion

commit v7 on v6

--- a/solution.py
+++ b/solution.py
@@ -278,7 +278,8 @@
     for b in range(4):
         limit = jnp.where(row_token == b, lengths_ref[b], limit)
     span = keys.shape[2]
-    order = [lax.rem(home + k, KEY_VALUE_HEADS) for k in (2, 1, 3, 0)]
+    turn_back = 2 * (lax.rem(chip, 8) // 4)
+    order = [lax.rem(home + k, KEY_VALUE_HEADS) for k in (2, 1 + turn_back, 3 - turn_back, 0)]
     for copy in swaps[2:4]:
         copy.wait_recv()
 
@@ -286,30 +287,41 @@
         g = order[k]
         q = q_bf[pl.ds(pl.multiple_of(rows * g, rows), rows), :]
         heads = pl.ds(pl.multiple_of(HEAD * g, HEAD), HEAD)
-        found = []
-        for c in range(2):
-            scores = jnp.zeros((rows, HEAD), F32)
-            for b in range(4):
-                part = lax.dot_general(
+        both = range(2)
+        parts = [
+            [
+                lax.dot_general(
                     q, keys[c, b, :, heads], (((1,), (1,)), ((), ())), preferred_element_type=F32
                 )
-                scores = jnp.where(row_token == b, part, scores)
-            scores = scores * inv
+                for b in range(4)
+            ]
+            for c in both
+        ]
+        tops, weighted, totals = [], [], []
+        for c in both:
+            scores = parts[c][0]
+            for b in range(1, 4):
+                scores = jnp.where(row_token == b, parts[c][b], scores)
             valid = (2 * chip + c) * span + wide_lane < limit
-            top = jnp.max(jnp.where(valid, scores, -1e30), axis=1, keepdims=True)
-            weights = jnp.where(valid, jnp.exp(scores - top), 0.0)
-            total = jnp.sum(weights, axis=1, keepdims=True)
-            rounded = weights.astype(BF16)
-            block = jnp.zeros((rows, HEAD), F32)
-            for b in range(4):
-                part = jnp.dot(rounded, values[c, b, :, heads], preferred_element_type=F32)
-                block = jnp.where(row_token == b, part, block)
-            found.append((top, total, block))
-        (m0, l0, o0), (m1, l1, o1) = found
-        top = jnp.maximum(m0, m1)
-        f0, f1 = jnp.exp(m0 - top), jnp.exp(m1 - top)
-        total = l0 * f0 + l1 * f1
-        block = o0 * f0 + o1 * f1
+            scores = jnp.where(valid, scores * inv, -1e30)
+            tops.append(jnp.max(scores, axis=1, keepdims=True))
+            weighted.append(jnp.where(valid, jnp.exp(scores - tops[c]), 0.0))
+        rounded = [weighted[c].astype(BF16) for c in both]
+        parts = [
+            [jnp.dot(rounded[c], values[c, b, :, heads], preferred_element_type=F32) for b in range(4)]
+            for c in both
+        ]
+        totals = [jnp.sum(weighted[c], axis=1, keepdims=True) for c in both]
+        top = jnp.maximum(tops[0], tops[1])
+        factors = [jnp.exp(tops[c] - top) for c in both]
+        total = totals[0] * factors[0] + totals[1] * factors[1]
+        blocks = []
+        for c in both:
+            block = parts[c][0]
+            for b in range(1, 4):
+                block = jnp.where(row_token == b, parts[c][b], block)
+            blocks.append(block * factors[c])
+        block = blocks[0] + blocks[1]
         stats = jnp.zeros((rows, HEAD), F32)
         for at, left in ((0, top), (3, total)):
             for i in range(3):

time: 86 us -> 83.7 us (0.973)
  Pallas kernels: 84.1 us -> 81.8 us
    pallas_call x1, Pallas kernels: 84.1 us -> 81.8 us  [on_device(): pl.pallas_call(functools.partial(kernel, chips), out_shape=(pltpu.VMEM(hi...]
where the time goes in v7:
time: 83.7 us; the launch traced here: 83.6 us
  Pallas kernels  81.8 us (98%)
  local copies, waits for them, and re-layouts  1.21 us (1%)
    pallas_call x1, Pallas kernels, on_device(): pl.pallas_call(functools.partial(kernel, chips), out_shape=(pltpu.VMEM(hi...  81.8 us

profile of v7, /device:TPU:37, one launch (start us, length us, event | category | flops | bytes accessed | tf_op | source)
XLA Modules:
  0.0 83.6 jit_solution(14698728061209614054)
XLA Ops:
  0.6 81.8 %shard_map.104 = (bf16[4,256]{1,0:T(4,128)(2,1)S(1)}, f32[8,128]{1,0:T(8,128)S(1)}) custom-call(s32[4]{0:T(128)} %lengths_hbm.1, s32[4]{0:T(128)} %positions_hbm.1, f32[1,128]{1,0:T(1,128)} %constant.2.clone.freq_hbm, bf16[4,256]{1,0:T(4,128)(2,1)} %hidden_hbm.1, bf16[256]{0:T(256)(128)(2,1)} %gain_hbm.1, bf16[144,16384]{1,0:T(8,128)(2,1)} %bitcast.1, ...), custom_call_target="tpu_custom_call" | custom-call | tf_op jit(solution)/shard_map/pallas_call | solution.py:482
  82.4 0.6 copy.12
  83.0 0.6 slice_reduce_fusion

commit v8 on v7

--- a/solution.py
+++ b/solution.py
@@ -188,7 +188,7 @@
         return total
 
     columns = w_qkv.shape[0]
-    proj = lax.fori_loop(0, chips, project, jnp.zeros((8, columns), F32), unroll=8)
+    proj = lax.fori_loop(0, chips, project, jnp.zeros((8, columns), F32), unroll=16)
     proj_ref[...] = jnp.zeros((8, 2 * HEAD), F32)
     proj_ref[:, :columns] = proj * scale[:, 0:1]
     wide = proj_ref[...]

time: 83.7 us -> 83.5 us (level)
  no operation moved by 1% of the time
where the time goes in v8:
time: 83.5 us; the launch traced here: 83.4 us
  Pallas kernels  81.6 us (98%)
  local copies, waits for them, and re-layouts  1.21 us (1%)
    pallas_call x1, Pallas kernels, on_device(): pl.pallas_call(functools.partial(kernel, chips), out_shape=(pltpu.VMEM(hi...  81.6 us

profile of v8, /device:TPU:37, one launch (start us, length us, event | category | flops | bytes accessed | tf_op | source)
XLA Modules:
  0.0 83.4 jit_solution(15217774711865662661)
XLA Ops:
  0.6 81.6 %shard_map.104 = (bf16[4,256]{1,0:T(4,128)(2,1)S(1)}, f32[8,128]{1,0:T(8,128)S(1)}) custom-call(s32[4]{0:T(128)} %lengths_hbm.1, s32[4]{0:T(128)} %positions_hbm.1, f32[1,128]{1,0:T(1,128)} %constant.2.clone.freq_hbm, bf16[4,256]{1,0:T(4,128)(2,1)} %hidden_hbm.1, bf16[256]{0:T(256)(128)(2,1)} %gain_hbm.1, bf16[144,16384]{1,0:T(8,128)(2,1)} %bitcast.1, ...), custom_call_target="tpu_custom_call" | custom-call | tf_op jit(solution)/shard_map/pallas_call | solution.py:482
  82.2 0.6 copy.12
  82.8 0.6 slice_reduce_fusion

commit v9 on v8

--- a/solution.py
+++ b/solution.py
@@ -438,10 +438,11 @@
     def _():
         await_bytes(slots4.at[pl.ds(0, 1)], recv_sem.at[3, 1])
 
-    def gather_sum(s, total):
-        return total + slots4[s].astype(F32)
-
-    result = lax.fori_loop(0, chips, gather_sum, zero, unroll=8)
+    def gather_sum(s, sums):
+        return tuple(total + slots4[4 * s + j].astype(F32) for j, total in enumerate(sums))
+
+    sums = lax.fori_loop(0, chips // 4, gather_sum, (zero,) * 4, unroll=2)
+    result = (sums[0] + sums[1]) + (sums[2] + sums[3])
     out_ref[:, :HEAD] = result[0:4, :].astype(BF16)
     out_ref[:, HEAD:] = half_turn(result)[0:4, :].astype(BF16)
 

time: 83.5 us -> 83.5 us (level)
  no operation moved by 1% of the time
where the time goes in v9:
time: 83.5 us; the launch traced here: 83.4 us
  Pallas kernels  81.5 us (98%)
  local copies, waits for them, and re-layouts  1.21 us (1%)
    pallas_call x1, Pallas kernels, on_device(): pl.pallas_call(functools.partial(kernel, chips), out_shape=(pltpu.VMEM(hi...  81.5 us

profile of v9, /device:TPU:37, one launch (start us, length us, event | category | flops | bytes accessed | tf_op | source)
XLA Modules:
  0.0 83.4 jit_solution(8122701796065314082)
XLA Ops:
  0.6 81.5 %shard_map.104 = (bf16[4,256]{1,0:T(4,128)(2,1)S(1)}, f32[8,128]{1,0:T(8,128)S(1)}) custom-call(s32[4]{0:T(128)} %lengths_hbm.1, s32[4]{0:T(128)} %positions_hbm.1, f32[1,128]{1,0:T(1,128)} %constant.2.clone.freq_hbm, bf16[4,256]{1,0:T(4,128)(2,1)} %hidden_hbm.1, bf16[256]{0:T(256)(128)(2,1)} %gain_hbm.1, bf16[144,16384]{1,0:T(8,128)(2,1)} %bitcast.1, ...), custom_call_target="tpu_custom_call" | custom-call | tf_op jit(solution)/shard_map/pallas_call | solution.py:483
  82.2 0.6 copy.12
  82.8 0.6 slice_reduce_fusion
